TPU v7x, 32 devices: a whole 2x2x4 slice. The times are simulated.
32 devices in a mesh: pipe: 4 (over z), expert: 4 (over y, x), tensor: 2 (over core).
Axes of the slice: x: 2, y: 2, z: 4, core: 2. Of those that a mesh axis runs over, the one named last changes fastest.
Arguments:
- inputs_prev: bfloat16 [4, 512, 3584], P('pipe', 'expert', 'tensor'), may hold values from -6 to 6
- cotangent_next: bfloat16 [4, 512, 3584], P('pipe', 'expert', 'tensor'), may hold values from -6 to 6
- saved_input: bfloat16 [4, 512, 3584], P('pipe', 'expert', 'tensor'), may hold values from -6 to 6
- expert_ids: int32 [2, 4, 512, 8], P(None, 'pipe', 'expert'), may hold values from 0 to 255, as said below
- keep_mask: int32 [2, 4, 512, 8], P(None, 'pipe', 'expert'), may hold values from 0 to 1, as said below
- slot_pos: int32 [2, 4, 512, 8], P(None, 'pipe', 'expert'), may hold values from 0 to 3, as said below
- weight_q: int32 [2, 4, 512, 8], P(None, 'pipe', 'expert'), may hold values from 1 to 4095
- gate_routed: bfloat16 [4, 4, 3584, 512], P('pipe', 'expert', None, 'tensor'), may hold values from -0.09375 to 0.09375
- up_routed: bfloat16 [4, 4, 3584, 512], P('pipe', 'expert', None, 'tensor'), may hold values from -0.09375 to 0.09375
- down_routed: bfloat16 [4, 4, 512, 3584], P('pipe', 'expert', 'tensor'), may hold values from -0.1875 to 0.1875
- gate_shared: bfloat16 [4, 3584, 1024], P('pipe', None, 'tensor'), may hold values from -0.09375 to 0.09375
- up_shared: bfloat16 [4, 3584, 1024], P('pipe', None, 'tensor'), may hold values from -0.09375 to 0.09375
- down_shared: bfloat16 [4, 1024, 3584], P('pipe', 'tensor'), may hold values from -0.1875 to 0.1875
Outputs:
- out_act: bfloat16 [4, 512, 3584], P('pipe', 'expert', 'tensor')
- in_grad: bfloat16 [4, 512, 3584], P('pipe', 'expert', 'tensor')
Inputs may be any that keep to these rules, and one draw needn't show every extreme that they name: `expert_ids`: each row names 8 different experts; in every section and micro-batch one expert below 2 is named by every row. `keep_mask`: 1 only where the expert named is below 2; in one block of 128 rows no expert has more than 4 kept choices, and in every section and micro-batch one expert has exactly 4 in every block. `slot_pos`: kept choices of one block naming the same expert hold different slots; 0 where keep_mask is 0.
All inputs are finite; a program needn't handle non-finite values.
Results may differ from a plain program's by a relative error of at most 0.005.
Values may be sent and summed in bfloat16 or wider, within the bound.
A program may use at most 64 MiB of HBM per device.

v0:
```python
import functools

import jax
import jax.numpy as jnp
from jax import lax
from jax.experimental import pallas as pl
from jax.experimental.pallas import tpu as pltpu
from jax.sharding import PartitionSpec as P

MESH = pl.DeviceIdType.MESH
ROW_CHUNKS = 4
F32 = jnp.float32
BF16 = jnp.bfloat16


def swish(values):
    return values * jax.nn.sigmoid(values)


def swish_slope(values):
    logistic = jax.nn.sigmoid(values)
    return logistic * (1.0 + values * (1.0 - logistic))


def dot(left, right):
    return jnp.dot(left, right, preferred_element_type=F32)


def contract_last(left, right):
    return lax.dot_general(left, right, (((1,), (1,)), ((), ())), preferred_element_type=F32)


def chunk_of(width):
    return 256 if width % 256 == 0 else 128


def kernel(
    sizes,
    x_prev, c_next, saved, ids, keep, slot, level,
    gate_r_hbm, up_r_hbm, down_r_hbm, gate_s_hbm, up_s_hbm, down_s_hbm,
    out_ref, grad_ref,
    gate_r, up_r, down_r, gate_s, up_s, down_s,
    full_x, full_c, full_s,
    a_saved, b_saved, hidden, grad_gate, grad_up,
    a_routed, b_routed,
    send_early, send_late, recv_early, recv_late, rows_early, rows_late,
    ret_send, ret_recv, ret_rows,
    part_out, part_grad, peer_out, peer_grad,
    weight_sem, saved_sem, saved_send, saved_recv,
    pipe_send, pipe_recv, fwd_send, fwd_recv,
    early_send, early_recv, late_send, late_recv, self_sem,
    ret_ssem, ret_rsem, part_send, part_recv,
):
    n_pipe, ne, nt, capacity = sizes
    tokens, width = x_prev.shape
    features = width * nt
    experts = ne // 2
    group = 2 * capacity
    me_p, me_e, me_t = lax.axis_index("pipe"), lax.axis_index("expert"), lax.axis_index("tensor")
    nxt, prv = lax.rem(me_p + 1, n_pipe), lax.rem(me_p + n_pipe - 1, n_pipe)
    my_cols = pl.ds(pl.multiple_of(me_t * width, 128), width)

    def peer_t(step):
        return lax.rem(me_t + step, nt)

    def peer_e(step):
        return lax.rem(me_e + step, ne)

    def remote(src, dst, ssem, rsem, device):
        return pltpu.make_async_remote_copy(
            src_ref=src, dst_ref=dst, send_sem=ssem, recv_sem=rsem,
            device_id=device, device_id_type=MESH,
        )

    saved_local = pltpu.make_async_copy(saved, full_s.at[:, my_cols], saved_sem)
    saved_local.start()
    loads = {}
    pairs = (
        (gate_s_hbm, gate_s), (up_s_hbm, up_s), (gate_r_hbm, gate_r),
        (up_r_hbm, up_r), (down_s_hbm, down_s), (down_r_hbm, down_r),
    )
    for n, (src, dst) in enumerate(pairs):
        loads[n] = pltpu.make_async_copy(src, dst, weight_sem.at[n])
        loads[n].start()

    barrier = pltpu.get_barrier_semaphore()
    greeted = [{"pipe": nxt}, {"pipe": prv}]
    for se in range(ne):
        for st in range(nt):
            if se or st:
                greeted.append({"expert": peer_e(se), "tensor": peer_t(st)})
    for device in greeted:
        pl.semaphore_signal(barrier, inc=1, device_id=device, device_id_type=MESH)
    pl.semaphore_wait(barrier, len(greeted))

    step_rows = tokens // ROW_CHUNKS
    pipe_copies = []
    for q in range(ROW_CHUNKS):
        rows = pl.ds(q * step_rows, step_rows)
        for a, (src, dst, to) in enumerate(((x_prev, full_x, nxt), (c_next, full_c, prv))):
            copy = remote(
                src.at[rows, :], dst.at[rows, my_cols],
                pipe_send.at[a, q], pipe_recv.at[a, q], {"pipe": to},
            )
            copy.start()
            pipe_copies.append(copy)
    saved_copies = []
    for st in range(1, nt):
        copy = remote(
            saved, full_s.at[:, my_cols], saved_send.at[st - 1], saved_recv.at[st - 1],
            {"tensor": peer_t(st)},
        )
        copy.start()
        saved_copies.append(copy)

    def targets(m):
        return jnp.where(keep[m] > 0, ids[m] * capacity + slot[m], -1)

    target_f, target_b = targets(0), targets(1)

    def table(target, values, slots_at):
        total = jnp.zeros((slots_at.shape[0], tokens), jnp.int32)
        for k in range(target.shape[0]):
            total = total + jnp.where(target[k:k + 1] == slots_at, values[k:k + 1], 0)
        return total

    used = experts * group
    place = lax.broadcasted_iota(jnp.int32, (used, tokens), 0)
    inside = lax.rem(place, group)
    owner = lax.div(place, group)
    slots_x = jnp.where(inside < capacity, owner * capacity + inside, -2)
    slots_c = jnp.where(inside >= capacity, owner * capacity + inside - capacity, -2)
    ones = jnp.ones(target_f.shape, jnp.int32)
    pick_x = table(target_f, ones, slots_x).astype(F32).astype(BF16)
    pick_c = table(target_b, ones, slots_c).astype(F32).astype(BF16)
    scale_c = jnp.sum(
        table(target_b, level[1], slots_c).astype(F32), axis=1, keepdims=True
    ) / 4096.0

    parts = ne * nt * group
    place = lax.broadcasted_iota(jnp.int32, (parts, tokens), 0)
    inside = lax.rem(place, group)
    owner = lax.div(place, 2 * nt * group)
    slots_o = jnp.where(inside < capacity, owner * capacity + inside, -2)
    slots_g = jnp.where(inside >= capacity, owner * capacity + inside - capacity, -2)
    level_o = table(target_f, level[0], slots_o)
    high = lax.div(level_o, 64)
    low = level_o - high * 64
    factor_high = (high.astype(F32) / 64.0).T.astype(BF16)
    factor_low = (low.astype(F32) / 4096.0).T.astype(BF16)
    factor_grad = table(target_b, ones, slots_g).astype(F32).T.astype(BF16)

    saved_local.wait()
    for copy in saved_copies:
        copy.wait_recv()
    cf = chunk_of(features)

    def exchange(buffer, landing, ssem, rsem, self_index):
        copies = []
        for se in range(1, ne):
            to = peer_e(se)
            copy = remote(
                buffer.at[lax.div(to, 2)], landing.at[me_e], ssem.at[se - 1], rsem.at[se - 1],
                {"expert": to},
            )
            copy.start()
            copies.append(copy)
        own = pltpu.make_async_copy(
            buffer.at[lax.div(me_e, 2)], landing.at[me_e], self_sem.at[self_index]
        )
        own.start()
        return copies, own

    def early_rows(n, carry):
        cols = pl.ds(pl.multiple_of(n * cf, 128), cf)
        picked = dot(pick_c, full_s[:, cols])
        for e in range(experts):
            send_early[e, :, cols] = picked[e * group:(e + 1) * group].astype(BF16)
        return carry

    lax.fori_loop(0, features // cf, early_rows, 0)
    early_copies, early_own = exchange(send_early, recv_early, early_send, early_recv, 0)

    def gather_rows(landing, dest):
        for i in range(0, ne, 2):
            both = jnp.concatenate(
                (landing[i].astype(F32), landing[i + 1].astype(F32)), axis=0
            )
            dest[i * group:(i + 2) * group, :] = both.astype(BF16)

    loads[0].wait()
    loads[1].wait()
    cs = chunk_of(gate_s.shape[1])

    def shared_saved(n, carry):
        cols = pl.ds(pl.multiple_of(n * cs, 128), cs)
        a_saved[:, cols] = dot(full_s[...], gate_s[:, cols])
        b_saved[:, cols] = dot(full_s[...], up_s[:, cols])
        return carry

    lax.fori_loop(0, gate_s.shape[1] // cs, shared_saved, 0)

    fwd_copies = []

    def forward(q):
        rows = pl.ds(q * step_rows, step_rows)
        for a, held in enumerate((full_x, full_c)):
            pipe_copies[2 * q + a].wait_recv()
            for st in range(1, nt):
                copy = remote(
                    held.at[rows, my_cols], held.at[rows, my_cols],
                    fwd_send.at[a, q, st - 1], fwd_recv.at[a, q, st - 1], {"tensor": peer_t(st)},
                )
                copy.start()
                fwd_copies.append(copy)

    for q in range(ROW_CHUNKS // 2):
        forward(q)

    for copy in early_copies:
        copy.wait_recv()
    early_own.wait()
    gather_rows(recv_early, rows_early)
    loads[2].wait()
    loads[3].wait()
    a_routed[...] = dot(rows_early[...], gate_r[...])
    b_routed[...] = dot(rows_early[...], up_r[...])

    for q in range(ROW_CHUNKS // 2, ROW_CHUNKS):
        forward(q)
    for copy in fwd_copies:
        copy.wait_recv()

    def late_rows(n, carry):
        cols = pl.ds(pl.multiple_of(n * cf, 128), cf)
        picked = dot(pick_x, full_x[:, cols]) + scale_c * dot(pick_c, full_c[:, cols])
        for e in range(experts):
            send_late[e, :, cols] = picked[e * group:(e + 1) * group].astype(BF16)
        return carry

    lax.fori_loop(0, features // cf, late_rows, 0)
    late_copies, late_own = exchange(send_late, recv_late, late_send, late_recv, 1)

    loads[4].wait()

    def shared_first(n, carry):
        cols = pl.ds(pl.multiple_of(n * cs, 128), cs)
        gate_pre = dot(full_x[...], gate_s[:, cols])
        up_pre = dot(full_x[...], up_s[:, cols])
        hidden[:, cols] = (swish(gate_pre) * up_pre).astype(BF16)
        grad_hidden = contract_last(full_c[...], down_s[cols, :])
        gate_back = a_saved[:, cols]
        grad_gate[:, cols] = (grad_hidden * b_saved[:, cols] * swish_slope(gate_back)).astype(BF16)
        grad_up[:, cols] = (grad_hidden * swish(gate_back)).astype(BF16)
        return carry

    lax.fori_loop(0, gate_s.shape[1] // cs, shared_first, 0)

    loads[5].wait()
    for copy in late_copies:
        copy.wait_recv()
    late_own.wait()
    gather_rows(recv_late, rows_late)
    gate_pre = dot(rows_late[...], gate_r[...])
    up_pre = dot(rows_late[...], up_r[...])
    grad_hidden = contract_last(rows_late[...], down_r[...])
    gate_back = a_routed[...]
    row = lax.broadcasted_iota(jnp.int32, gate_pre.shape, 0)
    ahead = lax.rem(row, group) < capacity
    hidden_r = jnp.where(ahead, swish(gate_pre) * up_pre, 0.0).astype(BF16)
    gate_grad_r = jnp.where(
        ahead, 0.0, grad_hidden * b_routed[...] * swish_slope(gate_back)
    ).astype(BF16)
    up_grad_r = jnp.where(ahead, 0.0, grad_hidden * swish(gate_back)).astype(BF16)
    cw = chunk_of(width)
    ret_copies = []
    for st in list(range(1, nt)) + [0]:
        to_t = peer_t(st)

        def routed_second(n, carry, to_t=to_t):
            at = pl.ds(pl.multiple_of(n * cw, 128), cw)
            cols = pl.ds(pl.multiple_of(to_t * width + n * cw, 128), cw)
            total = (
                dot(hidden_r, down_r[:, cols])
                + contract_last(gate_grad_r, gate_r[cols, :])
                + contract_last(up_grad_r, up_r[cols, :])
            )
            for i in range(ne):
                ret_send[i, to_t, :, at] = total[i * group:(i + 1) * group].astype(BF16)
            return carry

        lax.fori_loop(0, width // cw, routed_second, 0)
        for se in range(ne):
            if se or st:
                to_e = peer_e(se)
                n = se * nt + st - 1
                copy = remote(
                    ret_send.at[to_e, to_t], ret_recv.at[me_e, me_t],
                    ret_ssem.at[n], ret_rsem.at[n], {"expert": to_e, "tensor": to_t},
                )
                copy.start()
                ret_copies.append(copy)
    ret_own = pltpu.make_async_copy(
        ret_send.at[me_e, me_t], ret_recv.at[me_e, me_t], self_sem.at[2]
    )
    ret_own.start()

    part_copies = []
    for st in list(range(1, nt)) + [0]:
        to = peer_t(st)

        def shared_second(n, carry, st=st, to=to):
            at = pl.ds(pl.multiple_of(n * cw, 128), cw)
            cols = pl.ds(pl.multiple_of(to * width + n * cw, 128), cw)
            part_out[st, :, at] = dot(hidden[...], down_s[:, cols])
            part_grad[st, :, at] = contract_last(grad_gate[...], gate_s[cols, :]) + contract_last(
                grad_up[...], up_s[cols, :]
            )
            return carry

        lax.fori_loop(0, width // cw, shared_second, 0)
        if st:
            for a, (src, dst) in enumerate(((part_out, peer_out), (part_grad, peer_grad))):
                copy = remote(
                    src.at[st], dst.at[st - 1], part_send.at[a, st - 1], part_recv.at[a, st - 1],
                    {"tensor": to},
                )
                copy.start()
                part_copies.append(copy)

    for copy in ret_copies:
        copy.wait_recv()
    ret_own.wait()
    for i in range(0, ne * nt, 2):
        first, second = divmod(i, nt), divmod(i + 1, nt)
        both = jnp.concatenate((ret_recv[first].astype(F32), ret_recv[second].astype(F32)), axis=0)
        ret_rows[i * group:(i + 2) * group, :] = both.astype(BF16)
    for copy in part_copies:
        copy.wait_recv()

    def finish(n, carry):
        at = pl.ds(pl.multiple_of(n * cw, 128), cw)
        rows = ret_rows[:, at]
        out_sum = part_out[0, :, at] + (dot(factor_high, rows) + dot(factor_low, rows))
        grad_sum = part_grad[0, :, at] + dot(factor_grad, rows)
        for st in range(1, nt):
            out_sum = out_sum + peer_out[st - 1, :, at]
            grad_sum = grad_sum + peer_grad[st - 1, :, at]
        out_ref[:, at] = out_sum.astype(BF16)
        grad_ref[:, at] = grad_sum.astype(BF16)
        return carry

    lax.fori_loop(0, width // cw, finish, 0)

    for copy in (
        pipe_copies + saved_copies + fwd_copies + early_copies + late_copies + ret_copies
        + part_copies
    ):
        copy.wait_send()


def lanes_last(choices):
    return jnp.swapaxes(choices[:, 0], 1, 2)


def local(
    inputs_prev, cotangent_next, saved_input, expert_ids, keep_mask, slot_pos, weight_q,
    gate_routed, up_routed, down_routed, gate_shared, up_shared, down_shared,
):
    n_pipe, ne, nt = lax.axis_size("pipe"), lax.axis_size("expert"), lax.axis_size("tensor")
    tokens, width = inputs_prev.shape[1:]
    features = width * nt
    capacity = tokens // 32
    group = 2 * capacity
    experts = ne // 2
    fr, fs = gate_routed.shape[3], gate_shared.shape[2]
    vmem = pl.BlockSpec(memory_space=pltpu.VMEM)
    hbm = pl.BlockSpec(memory_space=pl.ANY)
    dma = pltpu.SemaphoreType.DMA
    shape = jax.ShapeDtypeStruct((tokens, width), BF16)
    out, grad = pl.pallas_call(
        functools.partial(kernel, (n_pipe, ne, nt, capacity)),
        out_shape=(shape, shape),
        in_specs=[hbm] * 3 + [vmem] * 4 + [hbm] * 6,
        out_specs=(vmem, vmem),
        scratch_shapes=[
            pltpu.VMEM((features, fr), BF16),
            pltpu.VMEM((features, fr), BF16),
            pltpu.VMEM((fr, features), BF16),
            pltpu.VMEM((features, fs), BF16),
            pltpu.VMEM((features, fs), BF16),
            pltpu.VMEM((fs, features), BF16),
            pltpu.VMEM((tokens, features), BF16),
            pltpu.VMEM((tokens, features), BF16),
            pltpu.VMEM((tokens, features), BF16),
            pltpu.VMEM((tokens, fs), F32),
            pltpu.VMEM((tokens, fs), F32),
            pltpu.VMEM((tokens, fs), BF16),
            pltpu.VMEM((tokens, fs), BF16),
            pltpu.VMEM((tokens, fs), BF16),
            pltpu.VMEM((ne * group, fr), F32),
            pltpu.VMEM((ne * group, fr), F32),
            pltpu.VMEM((experts, group, features), BF16),
            pltpu.VMEM((experts, group, features), BF16),
            pltpu.VMEM((ne, group, features), BF16),
            pltpu.VMEM((ne, group, features), BF16),
            pltpu.VMEM((ne * group, features), BF16),
            pltpu.VMEM((ne * group, features), BF16),
            pltpu.VMEM((ne, nt, group, width), BF16),
            pltpu.VMEM((ne, nt, group, width), BF16),
            pltpu.VMEM((ne * nt * group, width), BF16),
            pltpu.VMEM((nt, tokens, width), F32),
            pltpu.VMEM((nt, tokens, width), F32),
            pltpu.VMEM((nt - 1, tokens, width), F32),
            pltpu.VMEM((nt - 1, tokens, width), F32),
            dma((6,)),
            dma,
            dma((nt - 1,)),
            dma((nt - 1,)),
            dma((2, ROW_CHUNKS)),
            dma((2, ROW_CHUNKS)),
            dma((2, ROW_CHUNKS, nt - 1)),
            dma((2, ROW_CHUNKS, nt - 1)),
            dma((ne - 1,)),
            dma((ne - 1,)),
            dma((ne - 1,)),
            dma((ne - 1,)),
            dma((3,)),
            dma((ne * nt - 1,)),
            dma((ne * nt - 1,)),
            dma((2, nt - 1)),
            dma((2, nt - 1)),
        ],
        compiler_params=pltpu.CompilerParams(collective_id=0, has_side_effects=True),
        name="moe_step",
    )(
        inputs_prev[0], cotangent_next[0], saved_input[0],
        *(lanes_last(v) for v in (expert_ids, keep_mask, slot_pos, weight_q)),
        gate_routed[0, 0], up_routed[0, 0], down_routed[0, 0],
        gate_shared[0], up_shared[0], down_shared[0],
    )
    return out[None], grad[None]


def solution(mesh):
    return jax.shard_map(
        local,
        mesh=mesh,
        in_specs=(
            P("pipe", "expert", "tensor"),
            P("pipe", "expert", "tensor"),
            P("pipe", "expert", "tensor"),
            P(None, "pipe", "expert", None),
            P(None, "pipe", "expert", None),
            P(None, "pipe", "expert", None),
            P(None, "pipe", "expert", None),
            P("pipe", "expert", None, "tensor"),
            P("pipe", "expert", None, "tensor"),
            P("pipe", "expert", "tensor", None),
            P("pipe", None, "tensor"),
            P("pipe", None, "tensor"),
            P("pipe", "tensor", None),
        ),
        out_specs=(P("pipe", "expert", "tensor"), P("pipe", "expert", "tensor")),
        check_vma=False,
    )
```

profile of v0, /device:TPU:0, one launch (start us, length us, event | category | flops | bytes accessed | tf_op | source)
XLA Modules:
  0.0 51.4 jit_solution(8823779077847717748)
XLA Ops:
  0.6 47.2 %moe_step.1 = (bf16[128,1792]{1,0:T(8,128)(2,1)}, bf16[128,1792]{1,0:T(8,128)(2,1)}) custom-call(bf16[128,1792]{1,0:T(8,128)(2,1)} %bitcast.31, bf16[128,1792]{1,0:T(8,128)(2,1)} %bitcast.32, bf16[128,1792]{1,0:T(8,128)(2,1)} %bitcast.33, s32[2,8,128]{2,1,0:T(8,128)} %bitcast.34, s32[2,8,128]{2,1,0:T(8,128)} %bitcast.35, s32[2,8,128]{2,1,0:T(8,128)} %bitcast.36, ...), custom_call_target="tpu_custom_call" | custom-call | tf_op jit(solution)/shard_map/moe_step/pallas_call | solution.py:381
  47.8 1.8 %copy.17 = bf16[1,128,1792]{2,1,0:T(8,128)(2,1)} copy(bf16[1,128,1792]{2,1,0:T(8,128)(2,1)} %bitcast.30) | data formatting | bytes 917504
  49.6 1.8 %copy.18 = bf16[1,128,1792]{2,1,0:T(8,128)(2,1)} copy(bf16[1,128,1792]{2,1,0:T(8,128)(2,1)} %bitcast.29) | data formatting | bytes 917504
where the time goes:
time: 51.7 us; the launch traced here: 51.4 us
  Pallas kernels  47.2 us (91%)
  local copies, waits for them, and re-layouts  3.63 us (7%)
  between operations  0.64 us (1%)
    pallas_call x1, Pallas kernels, local(): pl.pallas_call(functools.partial(kernel, (n_pipe, ne, nt, capacity)), out...  47.2 us
    unnamed x2, local copies, waits for them, and re-layouts  3.63 us

commit v1 on v0

v1 whole, which is shorter than its diff:
```python
import functools

import jax
import jax.numpy as jnp
from jax import lax
from jax.experimental import pallas as pl
from jax.experimental.pallas import tpu as pltpu
from jax.sharding import PartitionSpec as P

MESH = pl.DeviceIdType.MESH
F32 = jnp.float32
BF16 = jnp.bfloat16
BLOCK = 8
LAST_COT = 2
INPUT_GATE = 4


def swish(values):
    return values * jax.nn.sigmoid(values)


def swish_slope(values):
    logistic = jax.nn.sigmoid(values)
    return logistic * (1.0 + values * (1.0 - logistic))


def dot(left, right):
    return jnp.dot(left, right, preferred_element_type=F32)


def contract_last(left, right):
    return lax.dot_general(left, right, (((1,), (1,)), ((), ())), preferred_element_type=F32)


def chunk_of(width):
    return 256 if width % 256 == 0 else 128


def kernel(
    sizes,
    x_hbm, c_hbm, saved_hbm, ids_hbm, keep_hbm, slot_hbm, level_hbm,
    gate_r_hbm, up_r_hbm, down_r_hbm, gate_s_hbm, up_s_hbm, down_s_hbm,
    out_ref, grad_ref,
    gate_r, up_r, down_r, gate_s, up_s, down_s, down_peer,
    tables, tables_next, x_own, c_own, full_x, full_c, full_s,
    a_saved, b_saved, gate_pre, up_pre, grad_hid, hidden, hidden_peer, grad_gate, grad_up,
    a_routed, b_routed,
    send_s, send_c, send_x, held_x, recv_s, recv_c, recv_x, rows,
    back_send_g, back_recv_g, back_send_o, back_recv_o, back_rows,
    part_grad, peer_grad, out_sum,
    weight_sem, table_sem, local_sem,
    next_send, next_recv, saved_send, saved_recv, down_send, down_recv,
    c_send, c_recv, x_send, x_recv, cf_send, cf_recv, xf_send, xf_recv,
    rs_send, rs_recv, rc_send, rc_recv, rx_send, rx_recv, pick_send, pick_recv,
    bg_send, bg_recv, bo_send, bo_recv, part_send, part_recv, hid_send, hid_recv,
):
    n_pipe, ne, nt, capacity = sizes
    tokens, width = x_own.shape
    features = width * nt
    blocks = send_s.shape[0]
    me_p, me_e, me_t = lax.axis_index("pipe"), lax.axis_index("expert"), lax.axis_index("tensor")
    nxt, prv = lax.rem(me_p + 1, n_pipe), lax.rem(me_p + n_pipe - 1, n_pipe)
    my_cols = pl.ds(pl.multiple_of(me_t * width, 128), width)
    cw = chunk_of(width)
    chunks = width // cw
    started = []

    def peer_t(step):
        return lax.rem(me_t + step, nt)

    def peer_e(step):
        return lax.rem(me_e + step, ne)

    def source_t(step):
        return lax.rem(me_t + nt - step, nt)

    def remote(src, dst, ssem, rsem, device):
        copy = pltpu.make_async_remote_copy(
            src_ref=src, dst_ref=dst, send_sem=ssem, recv_sem=rsem,
            device_id=device, device_id_type=MESH,
        )
        copy.start()
        started.append(copy)
        return copy

    def load(src, dst, sem):
        copy = pltpu.make_async_copy(src, dst, sem)
        copy.start()
        return copy

    def local_cols(n):
        return pl.ds(pl.multiple_of(n * cw, 128), cw)

    def cols_of(part, n):
        return pl.ds(pl.multiple_of(part * width + n * cw, 128), cw)

    table_loads = [
        load(src, tables.at[a], table_sem.at[a])
        for a, src in enumerate((ids_hbm, keep_hbm, slot_hbm, level_hbm))
    ]
    c_load = load(c_hbm, c_own, local_sem.at[0])
    saved_load = load(saved_hbm, full_s.at[:, my_cols], local_sem.at[1])
    x_load = load(x_hbm, x_own, local_sem.at[2])
    gate_s_load = load(gate_s_hbm, gate_s, weight_sem.at[0])
    up_s_load = load(up_s_hbm, up_s, weight_sem.at[1])
    gate_r_load = load(gate_r_hbm, gate_r, weight_sem.at[2])
    up_r_load = load(up_r_hbm, up_r, weight_sem.at[3])
    down_s_load = load(down_s_hbm, down_s, weight_sem.at[4])
    down_r_load = load(down_r_hbm, down_r, weight_sem.at[5])

    barrier = pltpu.get_barrier_semaphore()
    greeted = [{"pipe": nxt}, {"pipe": prv}]
    for se in range(ne):
        for st in range(nt):
            if se or st:
                greeted.append({"expert": peer_e(se), "tensor": peer_t(st)})
    for device in greeted:
        pl.semaphore_signal(barrier, inc=1, device_id=device, device_id_type=MESH)
    pl.semaphore_wait(barrier, len(greeted))

    for copy in table_loads:
        copy.wait()
    next_copies = [
        remote(tables.at[a, 0], tables_next.at[a], next_send.at[a], next_recv.at[a], {"pipe": prv})
        for a in range(3)
    ]

    def send_cot(n):
        return remote(
            c_own.at[:, local_cols(n)], full_c.at[:, cols_of(me_t, n)],
            c_send.at[n], c_recv.at[n], {"pipe": prv},
        )

    def send_in(n):
        return remote(
            x_own.at[:, local_cols(n)], full_x.at[:, cols_of(me_t, n)],
            x_send.at[n], x_recv.at[n], {"pipe": nxt},
        )

    c_load.wait()
    c_copies = [send_cot(n) for n in range(chunks - LAST_COT)]
    saved_load.wait()
    saved_copies = [
        remote(
            full_s.at[:, my_cols], full_s.at[:, my_cols], saved_send.at[st - 1],
            saved_recv.at[st - 1], {"tensor": peer_t(st)},
        )
        for st in range(1, nt)
    ]
    down_copies = []
    for st in range(1, nt):
        to = peer_t(st)
        down_copies.append(remote(
            down_s_hbm.at[:, pl.ds(pl.multiple_of(to * width, 128), width)], down_peer.at[st - 1],
            down_send.at[st - 1], down_recv.at[st - 1], {"tensor": to},
        ))

    def table(target, values, slots_at):
        total = jnp.zeros((slots_at.shape[0], tokens), jnp.int32)
        for k in range(target.shape[0]):
            total = total + jnp.where(target[k:k + 1] == slots_at, values[k:k + 1], 0)
        return total

    def targets(ids, keep, slot):
        return jnp.where(keep > 0, ids * capacity + slot, -1)

    target_f = targets(tables[0, 0], tables[1, 0], tables[2, 0])
    target_b = targets(tables[0, 1], tables[1, 1], tables[2, 1])
    level_f, level_b = tables[3, 0], tables[3, 1]
    used = max(16, blocks * BLOCK)
    place = lax.broadcasted_iota(jnp.int32, (used, tokens), 0)
    ones = jnp.ones(target_f.shape, jnp.int32)
    pick_b = table(target_b, ones, place).astype(F32).astype(BF16)
    scale_b = jnp.sum(table(target_b, level_b, place).astype(F32), axis=1, keepdims=True) / 4096.0

    def exchange(source_of, landing, ssem, rsem):
        copies = []
        for se in range(ne):
            for st in range(nt):
                if se or st:
                    to_e, n = peer_e(se), se * nt + st - 1
                    copies.append(remote(
                        source_of(to_e), landing.at[me_e, :, my_cols], ssem.at[n], rsem.at[n],
                        {"expert": to_e, "tensor": peer_t(st)},
                    ))
        return copies

    def block_of(e):
        return lax.div(lax.div(e, 2) * capacity, BLOCK)

    def keep_own(buffer, landing):
        landing[me_e, :, my_cols] = buffer[block_of(me_e)]

    def gather_rows(landing):
        for i in range(0, ne, 2):
            both = jnp.concatenate(
                (landing[i].astype(F32), landing[i + 1].astype(F32)), axis=0
            )
            rows[i * BLOCK:(i + 2) * BLOCK, :] = both.astype(BF16)

    def pick_rows(picks, scale, read, buffer, n):
        picked = dot(picks, read(n))
        if scale is not None:
            picked = picked * scale
        for b in range(blocks):
            buffer[b, :, local_cols(n)] = picked[b * BLOCK:(b + 1) * BLOCK].astype(BF16)

    def saved_rows(n, carry):
        pick_rows(pick_b, None, lambda m: full_s[:, cols_of(me_t, m)], send_s, n)
        return carry

    lax.fori_loop(0, chunks, saved_rows, 0)
    saved_row_copies = exchange(lambda e: send_s.at[block_of(e)], recv_s, rs_send, rs_recv)
    keep_own(send_s, recv_s)

    for copy in saved_copies:
        copy.wait_recv()
    gate_s_load.wait()
    up_s_load.wait()
    cs = chunk_of(gate_s.shape[1])

    def shared_saved(n, carry):
        cols = pl.ds(pl.multiple_of(n * cs, 128), cs)
        gate_back = dot(full_s[...], gate_s[:, cols])
        up_back = dot(full_s[...], up_s[:, cols])
        a_saved[:, cols] = up_back * swish_slope(gate_back)
        b_saved[:, cols] = swish(gate_back)
        return carry

    lax.fori_loop(0, gate_s.shape[1] // cs, shared_saved, 0)

    for copy in next_copies:
        copy.wait_recv()
    x_load.wait()
    target_n = targets(tables_next[0], tables_next[1], tables_next[2])
    pick_n = table(target_n, ones, place).astype(F32).astype(BF16)

    def input_rows(n, carry):
        pick_rows(pick_n, None, lambda m: x_own[:, local_cols(m)], send_x, n)
        return carry

    lax.fori_loop(0, chunks, input_rows, 0)
    picked_copy = remote(send_x, held_x, pick_send, pick_recv, {"pipe": nxt})
    c_copies += [send_cot(n) for n in range(chunks - LAST_COT, chunks)]

    for copy in saved_row_copies:
        copy.wait_recv()
    gather_rows(recv_s)
    gate_r_load.wait()
    up_r_load.wait()
    gate_back = dot(rows[...], gate_r[...])
    a_routed[...] = dot(rows[...], up_r[...]) * swish_slope(gate_back)
    b_routed[...] = swish(gate_back)

    down_s_load.wait()

    def forward(held, n, ssem, rsem):
        cols = cols_of(me_t, n)
        return [
            remote(
                held.at[:, cols], held.at[:, cols], ssem.at[n, st - 1], rsem.at[n, st - 1],
                {"tensor": peer_t(st)},
            )
            for st in range(1, nt)
        ]

    def add_cot(part, n, first=False):
        cols = cols_of(part, n)
        piece = contract_last(full_c[:, cols], down_s[:, cols])
        grad_hid[...] = piece if first else grad_hid[...] + piece

    def add_forwarded(copies, n, add):
        for st in range(1, nt):
            copies[st - 1].wait_recv()
            add(source_t(st), n)

    x_copies = []
    cf_copies = []
    for n in range(chunks):
        c_copies[n].wait_recv()
        cf_copies.append(forward(full_c, n, cf_send, cf_recv))
        if n == INPUT_GATE:
            x_copies = [send_in(m) for m in range(chunks)]
        pick_rows(pick_b, scale_b, lambda m: full_c[:, cols_of(me_t, m)], send_c, n)
        if n == chunks - 1:
            cot_row_copies = exchange(lambda e: send_c.at[block_of(e)], recv_c, rc_send, rc_recv)
        add_cot(me_t, n, first=n == 0)
        if n:
            add_forwarded(cf_copies[n - 1], n - 1, add_cot)
    keep_own(send_c, recv_c)
    add_forwarded(cf_copies[chunks - 1], chunks - 1, add_cot)

    grad_gate[...] = (grad_hid[...] * a_saved[...]).astype(BF16)
    grad_up[...] = (grad_hid[...] * b_saved[...]).astype(BF16)
    part_copies = []
    for st in list(range(1, nt)) + [0]:
        to = peer_t(st)

        def shared_back(n, carry, st=st, to=to):
            cols = cols_of(to, n)
            part_grad[st, :, local_cols(n)] = (
                contract_last(grad_gate[...], gate_s[cols, :])
                + contract_last(grad_up[...], up_s[cols, :])
            )
            return carry

        lax.fori_loop(0, chunks, shared_back, 0)
        if st:
            part_copies.append(remote(
                part_grad.at[st], peer_grad.at[st - 1], part_send.at[st - 1],
                part_recv.at[st - 1], {"tensor": to},
            ))

    picked_copy.wait_recv()
    input_row_copies = exchange(lambda e: held_x.at[block_of(e)], recv_x, rx_send, rx_recv)
    keep_own(held_x, recv_x)

    def send_back(total_of, buffer, landing, ssem, rsem):
        copies = []
        for st in list(range(1, nt)) + [0]:
            to_t = peer_t(st)

            def second(n, carry, to_t=to_t):
                total = total_of(cols_of(to_t, n))
                for i in range(ne):
                    buffer[i, to_t, :, local_cols(n)] = (
                        total[i * BLOCK:(i + 1) * BLOCK].astype(BF16)
                    )
                return carry

            lax.fori_loop(0, chunks, second, 0)
            for se in range(ne):
                if se or st:
                    to_e, n = peer_e(se), se * nt + st - 1
                    copies.append(remote(
                        buffer.at[to_e, to_t], landing.at[me_e, me_t], ssem.at[n], rsem.at[n],
                        {"expert": to_e, "tensor": to_t},
                    ))
        landing[me_e, me_t] = buffer[me_e, me_t]
        return copies

    for copy in cot_row_copies:
        copy.wait_recv()
    gather_rows(recv_c)
    down_r_load.wait()
    grad_back = contract_last(rows[...], down_r[...])
    gate_grad_r = (grad_back * a_routed[...]).astype(BF16)
    up_grad_r = (grad_back * b_routed[...]).astype(BF16)
    grad_back_copies = send_back(
        lambda cols: contract_last(gate_grad_r, gate_r[cols, :])
        + contract_last(up_grad_r, up_r[cols, :]),
        back_send_g, back_recv_g, bg_send, bg_recv,
    )

    for copy in input_row_copies:
        copy.wait_recv()
    gather_rows(recv_x)
    gate_fwd = dot(rows[...], gate_r[...])
    hidden_r = (swish(gate_fwd) * dot(rows[...], up_r[...])).astype(BF16)
    out_back_copies = send_back(
        lambda cols: dot(hidden_r, down_r[:, cols]), back_send_o, back_recv_o, bo_send, bo_recv
    )

    parts = ne * nt * BLOCK
    place_b = lax.broadcasted_iota(jnp.int32, (parts, tokens), 0)
    inside = lax.rem(place_b, BLOCK)
    expert = lax.div(lax.div(place_b, nt * BLOCK), 2)
    own = lax.div(inside, capacity) == lax.rem(expert, BLOCK // capacity)
    slots = jnp.where(own, expert * capacity + lax.rem(inside, capacity), -2)

    def gather_back(landing):
        for i in range(0, ne * nt, 2):
            first, second = divmod(i, nt), divmod(i + 1, nt)
            both = jnp.concatenate((landing[first].astype(F32), landing[second].astype(F32)), axis=0)
            back_rows[i * BLOCK:(i + 2) * BLOCK, :] = both.astype(BF16)

    def finish_grad():
        factor = table(target_b, ones, slots).astype(F32).T.astype(BF16)
        for copy in grad_back_copies:
            copy.wait_recv()
        gather_back(back_recv_g)
        for copy in part_copies:
            copy.wait_recv()

        def body(n, carry):
            at = local_cols(n)
            total = part_grad[0, :, at] + dot(factor, back_rows[:, at])
            for st in range(1, nt):
                total = total + peer_grad[st - 1, :, at]
            grad_ref[:, at] = total.astype(BF16)
            return carry

        lax.fori_loop(0, chunks, body, 0)

    def start_out():
        level = table(target_f, level_f, slots)
        high = lax.div(level, 64)
        low = level - high * 64
        factor_high = (high.astype(F32) / 64.0).T.astype(BF16)
        factor_low = (low.astype(F32) / 4096.0).T.astype(BF16)
        for copy in out_back_copies:
            copy.wait_recv()
        gather_back(back_recv_o)

        def body(n, carry):
            at = local_cols(n)
            out_sum[:, at] = dot(factor_high, back_rows[:, at]) + dot(factor_low, back_rows[:, at])
            return carry

        lax.fori_loop(0, chunks, body, 0)

    def add_in(part, n, first=False):
        cols = cols_of(part, n)
        piece = full_x[:, cols]
        gate_piece, up_piece = dot(piece, gate_s[cols, :]), dot(piece, up_s[cols, :])
        gate_pre[...] = gate_piece if first else gate_pre[...] + gate_piece
        up_pre[...] = up_piece if first else up_pre[...] + up_piece

    xf_copies = []
    for n in range(chunks):
        if n == chunks - 2:
            finish_grad()
        if n == chunks - 1:
            start_out()
            for copy in down_copies:
                copy.wait_recv()
        x_copies[n].wait_recv()
        xf_copies.append(forward(full_x, n, xf_send, xf_recv))
        add_in(me_t, n, first=n == 0)
        if n:
            add_forwarded(xf_copies[n - 1], n - 1, add_in)
    add_forwarded(xf_copies[chunks - 1], chunks - 1, add_in)

    hidden[...] = (swish(gate_pre[...]) * up_pre[...]).astype(BF16)
    hid_copies = [
        remote(
            hidden, hidden_peer.at[st - 1], hid_send.at[st - 1], hid_recv.at[st - 1],
            {"tensor": peer_t(st)},
        )
        for st in range(1, nt)
    ]

    def own_part(n, carry):
        at = local_cols(n)
        out_sum[:, at] = out_sum[:, at] + dot(hidden[...], down_s[:, cols_of(me_t, n)])
        return carry

    lax.fori_loop(0, chunks, own_part, 0)
    for copy in hid_copies:
        copy.wait_recv()

    def peer_part(n, carry):
        at = local_cols(n)
        total = out_sum[:, at]
        for st in range(1, nt):
            total = total + dot(hidden_peer[st - 1], down_peer[st - 1, :, at])
        out_ref[:, at] = total.astype(BF16)
        return carry

    lax.fori_loop(0, chunks, peer_part, 0)

    for copy in started:
        copy.wait_send()


def store(out, grad, out_hbm, grad_hbm, sem):
    first = pltpu.make_async_copy(out, out_hbm, sem.at[0])
    second = pltpu.make_async_copy(grad, grad_hbm, sem.at[1])
    first.start()
    second.start()
    first.wait()
    second.wait()


def lanes_last(choices):
    return jnp.swapaxes(choices[:, 0], 1, 2)


def in_hbm(values):
    return pltpu.with_memory_space_constraint(values, pltpu.HBM)


def local(
    inputs_prev, cotangent_next, saved_input, expert_ids, keep_mask, slot_pos, weight_q,
    gate_routed, up_routed, down_routed, gate_shared, up_shared, down_shared,
):
    n_pipe, ne, nt = lax.axis_size("pipe"), lax.axis_size("expert"), lax.axis_size("tensor")
    tokens, width = inputs_prev.shape[1:]
    topk = expert_ids.shape[3]
    features = width * nt
    capacity = tokens // 32
    experts = ne // 2
    blocks = -(-experts * capacity // BLOCK)
    fr, fs = gate_routed.shape[3], gate_shared.shape[2]
    chunks = width // chunk_of(width)
    peers = ne * nt - 1
    vmem = pl.BlockSpec(memory_space=pltpu.VMEM)
    hbm = pl.BlockSpec(memory_space=pl.ANY)
    dma = pltpu.SemaphoreType.DMA
    shape = pltpu.VMEM((tokens, width), BF16)
    out, grad = pl.pallas_call(
        functools.partial(kernel, (n_pipe, ne, nt, capacity)),
        out_shape=(shape, shape),
        in_specs=[hbm] * 13,
        out_specs=(vmem, vmem),
        scratch_shapes=[
            pltpu.VMEM((features, fr), BF16),
            pltpu.VMEM((features, fr), BF16),
            pltpu.VMEM((fr, features), BF16),
            pltpu.VMEM((features, fs), BF16),
            pltpu.VMEM((features, fs), BF16),
            pltpu.VMEM((fs, features), BF16),
            pltpu.VMEM((nt - 1, fs, width), BF16),
            pltpu.VMEM((4, 2, topk, tokens), jnp.int32),
            pltpu.VMEM((3, topk, tokens), jnp.int32),
            pltpu.VMEM((tokens, width), BF16),
            pltpu.VMEM((tokens, width), BF16),
            pltpu.VMEM((tokens, features), BF16),
            pltpu.VMEM((tokens, features), BF16),
            pltpu.VMEM((tokens, features), BF16),
            pltpu.VMEM((tokens, fs), F32),
            pltpu.VMEM((tokens, fs), F32),
            pltpu.VMEM((tokens, fs), F32),
            pltpu.VMEM((tokens, fs), F32),
            pltpu.VMEM((tokens, fs), F32),
            pltpu.VMEM((tokens, fs), BF16),
            pltpu.VMEM((nt - 1, tokens, fs), BF16),
            pltpu.VMEM((tokens, fs), BF16),
            pltpu.VMEM((tokens, fs), BF16),
            pltpu.VMEM((ne * BLOCK, fr), F32),
            pltpu.VMEM((ne * BLOCK, fr), F32),
            pltpu.VMEM((blocks, BLOCK, width), BF16),
            pltpu.VMEM((blocks, BLOCK, width), BF16),
            pltpu.VMEM((blocks, BLOCK, width), BF16),
            pltpu.VMEM((blocks, BLOCK, width), BF16),
            pltpu.VMEM((ne, BLOCK, features), BF16),
            pltpu.VMEM((ne, BLOCK, features), BF16),
            pltpu.VMEM((ne, BLOCK, features), BF16),
            pltpu.VMEM((ne * BLOCK, features), BF16),
            pltpu.VMEM((ne, nt, BLOCK, width), BF16),
            pltpu.VMEM((ne, nt, BLOCK, width), BF16),
            pltpu.VMEM((ne, nt, BLOCK, width), BF16),
            pltpu.VMEM((ne, nt, BLOCK, width), BF16),
            pltpu.VMEM((ne * nt * BLOCK, width), BF16),
            pltpu.VMEM((nt, tokens, width), F32),
            pltpu.VMEM((nt - 1, tokens, width), F32),
            pltpu.VMEM((tokens, width), F32),
            dma((6,)), dma((4,)), dma((3,)),
            dma((3,)), dma((3,)),
            dma((nt - 1,)), dma((nt - 1,)), dma((nt - 1,)), dma((nt - 1,)),
            dma((chunks,)), dma((chunks,)), dma((chunks,)), dma((chunks,)),
            dma((chunks, nt - 1)), dma((chunks, nt - 1)),
            dma((chunks, nt - 1)), dma((chunks, nt - 1)),
            dma((peers,)), dma((peers,)), dma((peers,)), dma((peers,)),
            dma((peers,)), dma((peers,)), dma, dma,
            dma((peers,)), dma((peers,)), dma((peers,)), dma((peers,)),
            dma((nt - 1,)), dma((nt - 1,)), dma((nt - 1,)), dma((nt - 1,)),
        ],
        compiler_params=pltpu.CompilerParams(
            collective_id=0, has_side_effects=True, vmem_limit_bytes=60 * 1024 * 1024
        ),
        name="moe_step",
    )(
        *(in_hbm(v) for v in (
            inputs_prev[0], cotangent_next[0], saved_input[0],
            *(lanes_last(v) for v in (expert_ids, keep_mask, slot_pos, weight_q)),
            gate_routed[0, 0], up_routed[0, 0], down_routed[0, 0],
            gate_shared[0], up_shared[0], down_shared[0],
        ))
    )
    result = jax.ShapeDtypeStruct((tokens, width), BF16)
    out, grad = pl.pallas_call(
        store,
        out_shape=(result, result),
        in_specs=[vmem] * 2,
        out_specs=(hbm, hbm),
        scratch_shapes=[dma((2,))],
        compiler_params=pltpu.CompilerParams(vmem_limit_bytes=2 * 1024 * 1024),
        name="store_out",
    )(*(pltpu.with_memory_space_constraint(v, pltpu.VMEM) for v in (out, grad)))
    return out[None], grad[None]


def solution(mesh):
    return jax.shard_map(
        local,
        mesh=mesh,
        in_specs=(
            P("pipe", "expert", "tensor"),
            P("pipe", "expert", "tensor"),
            P("pipe", "expert", "tensor"),
            P(None, "pipe", "expert", None),
            P(None, "pipe", "expert", None),
            P(None, "pipe", "expert", None),
            P(None, "pipe", "expert", None),
            P("pipe", "expert", None, "tensor"),
            P("pipe", "expert", None, "tensor"),
            P("pipe", "expert", "tensor", None),
            P("pipe", None, "tensor"),
            P("pipe", None, "tensor"),
            P("pipe", "tensor", None),
        ),
        out_specs=(P("pipe", "expert", "tensor"), P("pipe", "expert", "tensor")),
        check_vma=False,
    )
```

time: 51.7 us -> 45.5 us (0.88)
  local copies, waits for them, and re-layouts: 3.63 us -> 0 us
  Pallas kernels: 47.2 us -> 44.5 us
    unnamed x2 -> x0, local copies, waits for them, and re-layouts: 3.63 us -> none
    pallas_call x1, Pallas kernels: 47.2 us -> 43.5 us  [local(): pl.pallas_call(functools.partial(kernel, (n_pipe, ne, nt, capacity)), out...]
    pallas_call x0 -> x1, Pallas kernels: none -> 0.94 us  [local(): pl.pallas_call(store, out_shape=(result, result), in_specs=[vmem] * 2, ou...]
where the time goes in v1:
time: 45.5 us; the launch traced here: 45.1 us
  Pallas kernels  44.5 us (98%)
  between operations  0.64 us (1%)
    pallas_call x1, Pallas kernels, local(): pl.pallas_call(functools.partial(kernel, (n_pipe, ne, nt, capacity)), out...  43.5 us
    pallas_call x1, Pallas kernels, local(): pl.pallas_call(store, out_shape=(result, result), in_specs=[vmem] * 2, ou...  0.94 us

profile of v1, /device:TPU:0, one launch (start us, length us, event | category | flops | bytes accessed | tf_op | source)
XLA Modules:
  0.0 45.1 jit_solution(8198602726310852248)
XLA Ops:
  0.6 43.5 %moe_step.1 = (bf16[128,1792]{1,0:T(8,128)(2,1)S(1)}, bf16[128,1792]{1,0:T(8,128)(2,1)S(1)}) custom-call(bf16[128,1792]{1,0:T(8,128)(2,1)} %bitcast.29, bf16[128,1792]{1,0:T(8,128)(2,1)} %bitcast.30, bf16[128,1792]{1,0:T(8,128)(2,1)} %bitcast.31, s32[2,8,128]{2,1,0:T(8,128)} %bitcast.32, s32[2,8,128]{2,1,0:T(8,128)} %bitcast.33, s32[2,8,128]{2,1,0:T(8,128)} %bitcast.34, ...), custom_call_target="tpu_custom_call" | custom-call | tf_op jit(solution)/shard_map/moe_step/pallas_call | solution.py:501
  44.2 0.9 %store_out.1 = (bf16[128,1792]{1,0:T(8,128)(2,1)}, bf16[128,1792]{1,0:T(8,128)(2,1)}) custom-call(bf16[128,1792]{1,0:T(8,128)(2,1)S(1)} %get-tuple-element.6.out, bf16[128,1792]{1,0:T(8,128)(2,1)S(1)} %get-tuple-element.7.grad), custom_call_target="tpu_custom_call" | custom-call | tf_op jit(solution)/shard_map/store_out/pallas_call | solution.py:572

commit v2 on v1

v2 whole, which is shorter than its diff:
```python
import functools

import jax
import jax.numpy as jnp
from jax import lax
from jax.experimental import pallas as pl
from jax.experimental.pallas import tpu as pltpu
from jax.sharding import PartitionSpec as P

MESH = pl.DeviceIdType.MESH
F32 = jnp.float32
BF16 = jnp.bfloat16
BLOCK = 8
FIRST_COT = 3
EARLY_IN = 1
LATE = 2
RELAY_AT = 5
EARLY_TURNS = 2
INPUT_GATE = 3


def swish(values):
    return values * jax.nn.sigmoid(values)


def swish_slope(values):
    logistic = jax.nn.sigmoid(values)
    return logistic * (1.0 + values * (1.0 - logistic))


def dot(left, right):
    return jnp.dot(left, right, preferred_element_type=F32)


def contract_last(left, right):
    return lax.dot_general(left, right, (((1,), (1,)), ((), ())), preferred_element_type=F32)


def chunk_of(width):
    return 256 if width % 256 == 0 else 128


def kernel(
    sizes,
    x_hbm, c_hbm, saved_hbm, ids_hbm, keep_hbm, slot_hbm, level_hbm,
    gate_r_hbm, up_r_hbm, down_r_hbm, gate_s_hbm, up_s_hbm, down_s_hbm,
    out_ref, grad_ref,
    gate_r, up_r, down_r, gate_s, up_s, down_s, down_peer,
    tables, tables_next, x_own, c_own, full_x, full_c, full_s,
    a_saved, b_saved, grad_hid, pre, pre_peer, late, late_w, hidden, grad_gate, grad_up,
    a_routed, b_routed,
    send_s, send_c, send_x, held_x, relay_x, recv_s, recv_c, recv_x, rows,
    back_send_g, back_recv_g, back_send_o, back_recv_o, back_rows,
    gate_rt, up_rt, down_rt, gate_st, up_st,
    part_grad, peer_grad, out_sum, factor_high, factor_low, factor_grad,
    weight_sem, table_sem, local_sem,
    next_send, next_recv, saved_send, saved_recv, down_send, down_recv,
    c_send, c_recv, x_send, x_recv, cf_send, cf_recv, xf_send, xf_recv,
    rs_send, rs_recv, rc_send, rc_recv, rx_send, rx_recv, pick_send, pick_recv,
    bg_send, bg_recv, bo_send, bo_recv, part_send, part_recv, pre_send, pre_recv,
    late_send, late_recv,
):
    n_pipe, ne, nt, capacity = sizes
    tokens, width = x_own.shape
    features = width * nt
    experts, blocks = send_s.shape[0], send_x.shape[0]
    folds = width // send_s.shape[2]
    me_p, me_e, me_t = lax.axis_index("pipe"), lax.axis_index("expert"), lax.axis_index("tensor")
    nxt, prv = lax.rem(me_p + 1, n_pipe), lax.rem(me_p + n_pipe - 1, n_pipe)
    my_cols = pl.ds(pl.multiple_of(me_t * width, 128), width)
    cw = chunk_of(width)
    chunks = width // cw
    last_p = n_pipe - 1

    def peer_t(step):
        return lax.rem(me_t + step, nt)

    def peer_e(step):
        return lax.rem(me_e + step, ne)

    def source_t(step):
        return lax.rem(me_t + nt - step, nt)

    def planned(src, dst, ssem, rsem, device):
        return pltpu.make_async_remote_copy(
            src_ref=src, dst_ref=dst, send_sem=ssem, recv_sem=rsem,
            device_id=device, device_id_type=MESH,
        )

    def remote(src, dst, ssem, rsem, device):
        copy = planned(src, dst, ssem, rsem, device)
        copy.start()
        return copy

    def sent(whole, sem):
        planned(whole, whole, sem, sem, {"pipe": nxt}).wait_send()

    def received(whole, sem):
        planned(whole, whole, sem, sem, {"pipe": nxt}).wait_recv()

    def load(src, dst, sem):
        copy = pltpu.make_async_copy(src, dst, sem)
        copy.start()
        return copy

    def local_cols(n):
        return pl.ds(n * cw, cw)

    def cols_of(part, n):
        return pl.ds(pl.multiple_of(part * width + n * cw, 128), cw)

    c_load = load(c_hbm, c_own, local_sem.at[0])
    for a, src in enumerate((ids_hbm, keep_hbm, slot_hbm, level_hbm)):
        load(src, tables.at[a], table_sem)
    saved_load = load(saved_hbm, full_s.at[:, my_cols], local_sem.at[1])
    x_load = load(x_hbm, x_own, local_sem.at[2])

    barrier = pltpu.get_barrier_semaphore()
    greeted = [{"pipe": nxt}, {"pipe": prv}]
    for se in range(ne):
        for st in range(nt):
            if se or st:
                greeted.append({"expert": peer_e(se), "tensor": peer_t(st)})
    for device in greeted:
        pl.semaphore_signal(barrier, inc=1, device_id=device, device_id_type=MESH)
    c_load.wait()
    gate_s_load = load(gate_s_hbm, gate_s, weight_sem.at[0])
    up_s_load = load(up_s_hbm, up_s, weight_sem.at[1])
    gate_r_load = load(gate_r_hbm, gate_r, weight_sem.at[2])
    up_r_load = load(up_r_hbm, up_r, weight_sem.at[3])
    down_s_load = load(down_s_hbm, down_s, weight_sem.at[4])
    down_r_load = load(down_r_hbm, down_r, weight_sem.at[5])
    pl.semaphore_wait(barrier, len(greeted))

    pltpu.make_async_copy(tables, tables, table_sem).wait()
    for a in range(3):
        remote(tables.at[a, 0], tables_next.at[a], next_send, next_recv, {"pipe": prv})
    c_copies = [
        planned(
            c_own.at[:, local_cols(n)], full_c.at[:, cols_of(me_t, n)],
            c_send, c_recv.at[n], {"pipe": prv},
        )
        for n in range(chunks)
    ]
    x_copies = [
        planned(
            x_own.at[:, local_cols(n)], full_x.at[:, cols_of(me_t, n)],
            x_send, x_recv.at[n], {"pipe": nxt},
        )
        for n in range(chunks)
    ]
    for n in range(FIRST_COT):
        c_copies[n].start()
    saved_load.wait()
    x_load.wait()
    saved_copies = [
        remote(
            full_s.at[:, my_cols], full_s.at[:, my_cols], saved_send.at[st - 1],
            saved_recv.at[st - 1], {"tensor": peer_t(st)},
        )
        for st in range(1, nt)
    ]
    down_copies = []
    for st in range(1, nt):
        to = peer_t(st)
        down_copies.append(remote(
            down_s_hbm.at[:, pl.ds(pl.multiple_of(to * width, 128), width)], down_peer.at[st - 1],
            down_send.at[st - 1], down_recv.at[st - 1], {"tensor": to},
        ))
        for part in range(nt):
            at = pl.ds(part * width + (chunks - LATE) * cw, LATE * cw)
            for a, src in enumerate((gate_s_hbm, up_s_hbm)):
                remote(
                    src.at[at, :], late_w.at[a, st - 1, part], late_send, late_recv, {"tensor": to}
                )

    def table(target, values, slots_at):
        total = jnp.zeros((slots_at.shape[0], tokens), jnp.int32)
        for k in range(target.shape[0]):
            total = total + jnp.where(target[k:k + 1] == slots_at, values[k:k + 1], 0)
        return total

    def targets(ids, keep, slot):
        return jnp.where(keep > 0, ids * capacity + slot, -1)

    target_f = targets(tables[0, 0], tables[1, 0], tables[2, 0])
    target_b = targets(tables[0, 1], tables[1, 1], tables[2, 1])
    level_f, level_b = tables[3, 0], tables[3, 1]
    used = max(16, blocks * BLOCK)
    place = lax.broadcasted_iota(jnp.int32, (used, tokens), 0)
    ones = jnp.ones(target_f.shape, jnp.int32)
    pick_b = table(target_b, ones, place).astype(F32).astype(BF16)
    scale_b = jnp.sum(table(target_b, level_b, place).astype(F32), axis=1, keepdims=True) / 4096.0

    def pack(values):
        half = width // folds
        return jnp.concatenate((values[:, :half], values[:, width - half:]), axis=0).astype(BF16)

    def unpack(values):
        held = values.astype(F32)
        pieces = [held[f * capacity:(f + 1) * capacity] for f in range(folds)]
        return jnp.concatenate(pieces, axis=1)

    def exchange(buffer, landing, ssem, rsem):
        for se in range(ne):
            for st in range(nt):
                if se or st:
                    to_e, n = peer_e(se), min(se, 1)
                    remote(
                        buffer.at[lax.div(to_e, 2)], landing.at[me_e, me_t], ssem.at[n], rsem.at[n],
                        {"expert": to_e, "tensor": peer_t(st)},
                    )
        landing[me_e, me_t] = buffer[lax.div(me_e, 2)]

    def near(landing):
        return landing.at[0, pl.ds(0, nt - 1)]

    def far(landing):
        return landing.at[pl.ds(0, ne - 1)]

    def wait_rows(landing, rsem):
        received(near(landing), rsem.at[0])
        received(far(landing), rsem.at[1])

    def wait_rows_sent(landing, ssem):
        sent(near(landing), ssem.at[0])
        sent(far(landing), ssem.at[1])

    group = 16 // capacity

    def gather_rows(landing):
        for t in range(nt):
            for i in range(0, ne, group):
                held = [unpack(landing[j, t]) for j in range(i, i + group)]
                rows[i * capacity:(i + group) * capacity, t * width:(t + 1) * width] = (
                    jnp.concatenate(held, axis=0).astype(BF16)
                )

    def pick_rows(picks, read):
        return jnp.concatenate([dot(picks, read(n)) for n in range(chunks)], axis=1)

    def fill(buffer, picked):
        for k in range(experts):
            buffer[k] = pack(picked[k * capacity:(k + 1) * capacity])

    fill(send_s, pick_rows(pick_b, lambda n: full_s[:, cols_of(me_t, n)]))
    exchange(send_s, recv_s, rs_send, rs_recv)

    parts = ne * nt * capacity
    place_b = lax.broadcasted_iota(jnp.int32, (parts, tokens), 0)
    expert = lax.div(lax.div(place_b, nt * capacity), 2)
    slots = expert * capacity + lax.rem(place_b, capacity)
    level = table(target_f, level_f, slots)
    high = lax.div(level, 64)
    low = level - high * 64
    factor_high[...] = (high.astype(F32) / 64.0).T.astype(BF16)
    factor_low[...] = (low.astype(F32) / 4096.0).T.astype(BF16)
    factor_grad[...] = table(target_b, ones, slots).astype(F32).T.astype(BF16)

    for copy in saved_copies:
        copy.wait_recv()
    gate_s_load.wait()
    up_s_load.wait()
    cs = chunk_of(gate_s.shape[1])

    for n in range(gate_s.shape[1] // cs):
        cols = pl.ds(n * cs, cs)
        gate_back = dot(full_s[...], gate_s[:, cols])
        up_back = dot(full_s[...], up_s[:, cols])
        a_saved[:, cols] = up_back * swish_slope(gate_back)
        b_saved[:, cols] = swish(gate_back)

    received(tables_next, next_recv)
    target_n = targets(tables_next[0], tables_next[1], tables_next[2])
    pick_n = table(target_n, ones, place).astype(F32).astype(BF16)

    picked = pick_rows(pick_n, lambda n: x_own[:, local_cols(n)])
    for b in range(blocks):
        send_x[b] = picked[b * BLOCK:(b + 1) * BLOCK].astype(BF16)
    picked_copy = remote(send_x, held_x, pick_send, pick_recv, {"pipe": nxt})

    order = [(c_copies, n) for n in range(FIRST_COT, chunks)]
    early = list(order)
    for m in range(EARLY_IN):
        early.insert(len(early) - 2 * EARLY_IN + 1 + 2 * m, (x_copies, m))

    @pl.when(me_p == last_p)
    def _():
        for kind, n in early:
            kind[n].start()

    @pl.when(me_p != last_p)
    def _():
        for kind, n in order:
            kind[n].start()

    for load_done in (gate_r_load, up_r_load, down_r_load):
        load_done.wait()
    turned = features // chunks

    def turn(n):
        at = pl.ds(n * turned, turned)
        gate_st[:, at] = gate_s[at, :].T
        up_st[:, at] = up_s[at, :].T
        gate_rt[:, at] = gate_r[at, :].T
        up_rt[:, at] = up_r[at, :].T
        down_rt[at, :] = down_r[:, at].T

    for n in range(EARLY_TURNS):
        turn(n)

    wait_rows(recv_s, rs_recv)
    gather_rows(recv_s)
    gate_back = dot(rows[...], gate_r[...])
    a_routed[...] = dot(rows[...], up_r[...]) * swish_slope(gate_back)
    b_routed[...] = swish(gate_back)

    down_s_load.wait()

    def forward(held, n, ssem, rsem):
        cols = cols_of(me_t, n)
        return [
            remote(
                held.at[:, cols], held.at[:, cols], ssem.at[st - 1], rsem.at[n, st - 1],
                {"tensor": peer_t(st)},
            )
            for st in range(1, nt)
        ]

    def add_cot(part, n, first=False):
        cols = cols_of(part, n)
        piece = contract_last(full_c[:, cols], down_s[:, cols])
        grad_hid[...] = piece if first else grad_hid[...] + piece

    def add_forwarded(copies, n, add):
        for st in range(1, nt):
            copies[st - 1].wait_recv()
            add(source_t(st), n)

    cf_copies = []
    for n in range(chunks):
        c_copies[n].wait_recv()
        cf_copies.append(forward(full_c, n, cf_send, cf_recv))
        if n == INPUT_GATE:
            @pl.when(me_p != last_p)
            def _():
                for m in range(EARLY_IN):
                    x_copies[m].start()

            for m in range(EARLY_IN, chunks):
                x_copies[m].start()
        if n == chunks - 1:
            fill(send_c, scale_b * pick_rows(pick_b, lambda m: full_c[:, cols_of(me_t, m)]))
            exchange(send_c, recv_c, rc_send, rc_recv)
        if n == RELAY_AT:
            picked_copy.wait_recv()
            for k in range(experts):
                b, at = divmod(k * capacity, BLOCK)
                relay_x[k] = pack(held_x[b].astype(F32)[at:at + capacity])
            exchange(relay_x, recv_x, rx_send, rx_recv)
        add_cot(me_t, n, first=n == 0)
        if n + EARLY_TURNS < chunks:
            turn(n + EARLY_TURNS)
        if n:
            add_forwarded(cf_copies[n - 1], n - 1, add_cot)
    xf_copies = []

    def land_in(n):
        x_copies[n].wait_recv()
        xf_copies.append(forward(full_x, n, xf_send, xf_recv))

    def send_back(total_of, buffer, landing, ssem, rsem):
        for st in list(range(1, nt)) + [0]:
            to_t = peer_t(st)
            total = jnp.concatenate([total_of(cols_of(to_t, n)) for n in range(chunks)], axis=1)
            for i in range(ne):
                buffer[i, to_t] = pack(total[i * capacity:(i + 1) * capacity])
            for se in range(ne):
                if se or st:
                    to_e, n = peer_e(se), min(se, 1)
                    remote(
                        buffer.at[to_e, to_t], landing.at[me_e, me_t], ssem.at[n], rsem.at[n],
                        {"expert": to_e, "tensor": to_t},
                    )
        landing[me_e, me_t] = buffer[me_e, me_t]

    add_forwarded(cf_copies[chunks - 1], chunks - 1, add_cot)
    grad_gate[...] = (grad_hid[...] * a_saved[...]).astype(BF16)
    grad_up[...] = (grad_hid[...] * b_saved[...]).astype(BF16)
    part_copies = []
    for st in list(range(1, nt)) + [0]:
        to = peer_t(st)
        for n in range(chunks):
            cols = cols_of(to, n)
            part_grad[st, :, local_cols(n)] = (
                dot(grad_gate[...], gate_st[:, cols]) + dot(grad_up[...], up_st[:, cols])
            )
        if st:
            part_copies.append(remote(
                part_grad.at[st], peer_grad.at[st - 1], part_send.at[st - 1],
                part_recv.at[st - 1], {"tensor": to},
            ))
    land_in(0)

    wait_rows(recv_x, rx_recv)
    gather_rows(recv_x)
    gate_fwd = dot(rows[...], gate_r[...])
    hidden_r = (swish(gate_fwd) * dot(rows[...], up_r[...])).astype(BF16)
    send_back(
        lambda cols: dot(hidden_r, down_r[:, cols]), back_send_o, back_recv_o, bo_send, bo_recv
    )
    wait_rows(recv_c, rc_recv)
    gather_rows(recv_c)
    grad_back = dot(rows[...], down_rt[...])
    gate_grad_r = (grad_back * a_routed[...]).astype(BF16)
    up_grad_r = (grad_back * b_routed[...]).astype(BF16)
    send_back(
        lambda cols: dot(gate_grad_r, gate_rt[:, cols]) + dot(up_grad_r, up_rt[:, cols]),
        back_send_g, back_recv_g, bg_send, bg_recv,
    )
    land_in(1)

    land_in(2)

    def gather_back(landing):
        for i in range(0, ne * nt, group):
            held = [unpack(landing[divmod(j, nt)]) for j in range(i, i + group)]
            back_rows[i * capacity:(i + group) * capacity, :] = (
                jnp.concatenate(held, axis=0).astype(BF16)
            )

    def finish_grad():
        wait_rows(back_recv_g, bg_recv)
        gather_back(back_recv_g)
        for copy in part_copies:
            copy.wait_recv()

        for n in range(chunks):
            at = local_cols(n)
            total = part_grad[0, :, at] + dot(factor_grad[...], back_rows[:, at])
            for st in range(1, nt):
                total = total + peer_grad[st - 1, :, at]
            grad_ref[:, at] = total.astype(BF16)

    early_n = chunks - LATE

    def arrived(n):
        for copy in xf_copies[n]:
            copy.wait_recv()

    def add_in(spans, first=False):
        for a, weight in enumerate((gate_s, up_s)):
            piece = 0.0
            for part, n in spans:
                cols = cols_of(part, n)
                piece = piece + dot(full_x[:, cols], weight[cols, :])
            pre[a] = piece if first else pre[a] + piece

    for n in range(3, early_n - 1):
        land_in(n)
    for n in range(early_n - 1):
        arrived(n)
    add_in([(source_t(st), n) for n in range(early_n - 1) for st in range(nt)], first=True)
    land_in(early_n - 1)
    land_in(early_n)
    add_in([(me_t, early_n - 1)])
    arrived(early_n - 1)
    add_in([(source_t(st), early_n - 1) for st in range(1, nt)])

    pre_copies = [
        remote(
            pre, pre_peer.at[st - 1], pre_send.at[st - 1], pre_recv.at[st - 1],
            {"tensor": peer_t(st)},
        )
        for st in range(1, nt)
    ]
    wait_rows(back_recv_o, bo_recv)
    gather_back(back_recv_o)
    for n in range(chunks):
        at = local_cols(n)
        held = back_rows[:, at]
        out_sum[:, at] = dot(factor_high[...], held) + dot(factor_low[...], held)
    finish_grad()
    for copy in down_copies:
        copy.wait_recv()
    received(late_w, late_recv)
    sent(c_own, c_send)
    sent(tables_next, next_send)
    sent(send_x, pick_send)
    for landing, sem in (
        (recv_s, rs_send), (recv_c, rc_send), (recv_x, rx_send),
        (back_recv_g, bg_send), (back_recv_o, bo_send),
    ):
        wait_rows_sent(landing, sem)
    sent(late_w, late_send)
    for copy in saved_copies + down_copies + part_copies:
        copy.wait_send()
    for st in range(1, nt):
        sent(full_c.at[:, my_cols], cf_send.at[st - 1])
    def late_piece(unit, a, part, n):
        cols = cols_of(part, n)
        if unit:
            at = (n - early_n) * cw
            return dot(full_x[:, cols], late_w[a, unit - 1, part, at:at + cw, :])
        return dot(full_x[:, cols], (gate_s, up_s)[a][cols, :])

    for n in range(early_n, chunks - 1):
        arrived(n)
    for unit in range(nt):
        for a in range(2):
            total = pre[a] if unit == 0 else 0.0
            for n in range(early_n, chunks - 1):
                for st in range(nt):
                    total = total + late_piece(unit, a, source_t(st), n)
            late[unit, a] = total
    land_in(chunks - 1)
    for unit in range(nt):
        for a in range(2):
            late[unit, a] = late[unit, a] + late_piece(unit, a, me_t, chunks - 1)
    for copy in pre_copies:
        copy.wait_recv()
    arrived(chunks - 1)
    for unit in range(nt):
        total = [late[unit, 0], late[unit, 1]]
        for a in range(2):
            if unit:
                total[a] = total[a] + pre_peer[unit - 1, a]
            for st in range(1, nt):
                total[a] = total[a] + late_piece(unit, a, source_t(st), chunks - 1)
        hidden[unit] = (swish(total[0]) * total[1]).astype(BF16)
    for n in range(chunks):
        at = local_cols(n)
        total = out_sum[:, at] + dot(hidden[0], down_s[:, cols_of(me_t, n)])
        for st in range(1, nt):
            total = total + dot(hidden[st], down_peer[st - 1, :, at])
        out_ref[:, at] = total.astype(BF16)

    sent(x_own, x_send)
    for st in range(1, nt):
        sent(full_x.at[:, my_cols], xf_send.at[st - 1])
    for copy in pre_copies:
        copy.wait_send()


def store(out, grad, out_hbm, grad_hbm, sem):
    first = pltpu.make_async_copy(out, out_hbm, sem.at[0])
    second = pltpu.make_async_copy(grad, grad_hbm, sem.at[1])
    first.start()
    second.start()
    first.wait()
    second.wait()


def lanes_last(choices):
    return jnp.swapaxes(choices[:, 0], 1, 2)


def in_hbm(values):
    return pltpu.with_memory_space_constraint(values, pltpu.HBM)


def local(
    inputs_prev, cotangent_next, saved_input, expert_ids, keep_mask, slot_pos, weight_q,
    gate_routed, up_routed, down_routed, gate_shared, up_shared, down_shared,
):
    n_pipe, ne, nt = lax.axis_size("pipe"), lax.axis_size("expert"), lax.axis_size("tensor")
    tokens, width = inputs_prev.shape[1:]
    topk = expert_ids.shape[3]
    features = width * nt
    capacity = tokens // 32
    experts = ne // 2
    blocks = -(-experts * capacity // BLOCK)
    folded = width // 2 if width % 256 == 0 else width
    fr, fs = gate_routed.shape[3], gate_shared.shape[2]
    chunks = width // chunk_of(width)
    peers = ne * nt - 1
    vmem = pl.BlockSpec(memory_space=pltpu.VMEM)
    hbm = pl.BlockSpec(memory_space=pl.ANY)
    dma = pltpu.SemaphoreType.DMA
    shape = pltpu.VMEM((tokens, width), BF16)
    out, grad = pl.pallas_call(
        functools.partial(kernel, (n_pipe, ne, nt, capacity)),
        out_shape=(shape, shape),
        in_specs=[hbm] * 13,
        out_specs=(vmem, vmem),
        scratch_shapes=[
            pltpu.VMEM((features, fr), BF16),
            pltpu.VMEM((features, fr), BF16),
            pltpu.VMEM((fr, features), BF16),
            pltpu.VMEM((features, fs), BF16),
            pltpu.VMEM((features, fs), BF16),
            pltpu.VMEM((fs, features), BF16),
            pltpu.VMEM((nt - 1, fs, width), BF16),
            pltpu.VMEM((4, 2, topk, tokens), jnp.int32),
            pltpu.VMEM((3, topk, tokens), jnp.int32),
            pltpu.VMEM((tokens, width), BF16),
            pltpu.VMEM((tokens, width), BF16),
            pltpu.VMEM((tokens, features), BF16),
            pltpu.VMEM((tokens, features), BF16),
            pltpu.VMEM((tokens, features), BF16),
            pltpu.VMEM((tokens, fs), F32),
            pltpu.VMEM((tokens, fs), F32),
            pltpu.VMEM((tokens, fs), F32),
            pltpu.VMEM((2, tokens, fs), F32),
            pltpu.VMEM((nt - 1, 2, tokens, fs), F32),
            pltpu.VMEM((nt, 2, tokens, fs), F32),
            pltpu.VMEM((2, nt - 1, nt, LATE * chunk_of(width), fs), BF16),
            pltpu.VMEM((nt, tokens, fs), BF16),
            pltpu.VMEM((tokens, fs), BF16),
            pltpu.VMEM((tokens, fs), BF16),
            pltpu.VMEM((ne * capacity, fr), F32),
            pltpu.VMEM((ne * capacity, fr), F32),
            pltpu.VMEM((experts, BLOCK, folded), BF16),
            pltpu.VMEM((experts, BLOCK, folded), BF16),
            pltpu.VMEM((blocks, BLOCK, width), BF16),
            pltpu.VMEM((blocks, BLOCK, width), BF16),
            pltpu.VMEM((experts, BLOCK, folded), BF16),
            pltpu.VMEM((ne, nt, BLOCK, folded), BF16),
            pltpu.VMEM((ne, nt, BLOCK, folded), BF16),
            pltpu.VMEM((ne, nt, BLOCK, folded), BF16),
            pltpu.VMEM((ne * capacity, features), BF16),
            pltpu.VMEM((ne, nt, BLOCK, folded), BF16),
            pltpu.VMEM((ne, nt, BLOCK, folded), BF16),
            pltpu.VMEM((ne, nt, BLOCK, folded), BF16),
            pltpu.VMEM((ne, nt, BLOCK, folded), BF16),
            pltpu.VMEM((ne * nt * capacity, width), BF16),
            pltpu.VMEM((fr, features), BF16),
            pltpu.VMEM((fr, features), BF16),
            pltpu.VMEM((features, fr), BF16),
            pltpu.VMEM((fs, features), BF16),
            pltpu.VMEM((fs, features), BF16),
            pltpu.VMEM((nt, tokens, width), F32),
            pltpu.VMEM((nt - 1, tokens, width), F32),
            pltpu.VMEM((tokens, width), F32),
            pltpu.VMEM((tokens, ne * nt * capacity), BF16),
            pltpu.VMEM((tokens, ne * nt * capacity), BF16),
            pltpu.VMEM((tokens, ne * nt * capacity), BF16),
            dma((6,)), dma, dma((3,)),
            dma, dma,
            dma((nt - 1,)), dma((nt - 1,)), dma((nt - 1,)), dma((nt - 1,)),
            dma, dma((chunks,)), dma, dma((chunks,)),
            dma((nt - 1,)), dma((chunks, nt - 1)),
            dma((nt - 1,)), dma((chunks, nt - 1)),
            dma((2,)), dma((2,)), dma((2,)), dma((2,)),
            dma((2,)), dma((2,)), dma, dma,
            dma((2,)), dma((2,)), dma((2,)), dma((2,)),
            dma((nt - 1,)), dma((nt - 1,)), dma((nt - 1,)), dma((nt - 1,)),
            dma, dma,
        ],
        compiler_params=pltpu.CompilerParams(
            collective_id=0, has_side_effects=True, vmem_limit_bytes=60 * 1024 * 1024
        ),
        name="moe_step",
    )(
        *(in_hbm(v) for v in (
            inputs_prev[0], cotangent_next[0], saved_input[0],
            *(lanes_last(v) for v in (expert_ids, keep_mask, slot_pos, weight_q)),
            gate_routed[0, 0], up_routed[0, 0], down_routed[0, 0],
            gate_shared[0], up_shared[0], down_shared[0],
        ))
    )
    result = jax.ShapeDtypeStruct((tokens, width), BF16)
    out, grad = pl.pallas_call(
        store,
        out_shape=(result, result),
        in_specs=[vmem] * 2,
        out_specs=(hbm, hbm),
        scratch_shapes=[dma((2,))],
        compiler_params=pltpu.CompilerParams(vmem_limit_bytes=2 * 1024 * 1024),
        name="store_out",
    )(*(pltpu.with_memory_space_constraint(v, pltpu.VMEM) for v in (out, grad)))
    return out[None], grad[None]


def solution(mesh):
    return jax.shard_map(
        local,
        mesh=mesh,
        in_specs=(
            P("pipe", "expert", "tensor"),
            P("pipe", "expert", "tensor"),
            P("pipe", "expert", "tensor"),
            P(None, "pipe", "expert", None),
            P(None, "pipe", "expert", None),
            P(None, "pipe", "expert", None),
            P(None, "pipe", "expert", None),
            P("pipe", "expert", None, "tensor"),
            P("pipe", "expert", None, "tensor"),
            P("pipe", "expert", "tensor", None),
            P("pipe", None, "tensor"),
            P("pipe", None, "tensor"),
            P("pipe", "tensor", None),
        ),
        out_specs=(P("pipe", "expert", "tensor"), P("pipe", "expert", "tensor")),
        check_vma=False,
    )
```

time: 45.5 us -> 33.9 us (0.75)
  Pallas kernels: 44.5 us -> 33.1 us
    pallas_call x1, Pallas kernels: 43.5 us -> 32.2 us  [local(): pl.pallas_call(functools.partial(kernel, (n_pipe, ne, nt, capacity)), out...]
where the time goes in v2:
time: 33.9 us; the launch traced here: 33.8 us
  Pallas kernels  33.1 us (98%)
  between operations  0.64 us (2%)
    pallas_call x1, Pallas kernels, local(): pl.pallas_call(functools.partial(kernel, (n_pipe, ne, nt, capacity)), out...  32.2 us
    pallas_call x1, Pallas kernels, local(): pl.pallas_call(store, out_shape=(result, result), in_specs=[vmem] * 2, ou...  0.94 us

profile of v2, /device:TPU:0, one launch (start us, length us, event | category | flops | bytes accessed | tf_op | source)
XLA Modules:
  0.0 33.8 jit_solution(10206467877734133551)
XLA Ops:
  0.6 32.2 %moe_step.1 = (bf16[128,1792]{1,0:T(8,128)(2,1)S(1)}, bf16[128,1792]{1,0:T(8,128)(2,1)S(1)}) custom-call(bf16[128,1792]{1,0:T(8,128)(2,1)} %bitcast.29, bf16[128,1792]{1,0:T(8,128)(2,1)} %bitcast.30, bf16[128,1792]{1,0:T(8,128)(2,1)} %bitcast.31, s32[2,8,128]{2,1,0:T(8,128)} %bitcast.32, s32[2,8,128]{2,1,0:T(8,128)} %bitcast.33, s32[2,8,128]{2,1,0:T(8,128)} %bitcast.34, ...), custom_call_target="tpu_custom_call" | custom-call | tf_op jit(solution)/shard_map/moe_step/pallas_call | solution.py:581
  32.8 0.9 %store_out.1 = (bf16[128,1792]{1,0:T(8,128)(2,1)}, bf16[128,1792]{1,0:T(8,128)(2,1)}) custom-call(bf16[128,1792]{1,0:T(8,128)(2,1)S(1)} %get-tuple-element.6.out, bf16[128,1792]{1,0:T(8,128)(2,1)S(1)} %get-tuple-element.7.grad), custom_call_target="tpu_custom_call" | custom-call | tf_op jit(solution)/shard_map/store_out/pallas_call | solution.py:663

commit v3 on v2

--- a/solution.py
+++ b/solution.py
@@ -47,24 +47,23 @@
     out_ref, grad_ref,
     gate_r, up_r, down_r, gate_s, up_s, down_s, down_peer,
     tables, tables_next, x_own, c_own, full_x, full_c, full_s,
-    a_saved, b_saved, grad_hid, pre, pre_peer, late, late_w, hidden, grad_gate, grad_up,
+    a_saved, b_saved, grad_hid, pre, pre_peer, late, late_w, hidden, drain, grad_gate, grad_up,
     a_routed, b_routed,
     send_s, send_c, send_x, held_x, relay_x, recv_s, recv_c, recv_x, rows,
     back_send_g, back_recv_g, back_send_o, back_recv_o, back_rows,
     gate_rt, up_rt, down_rt, gate_st, up_st,
     part_grad, peer_grad, out_sum, factor_high, factor_low, factor_grad,
-    weight_sem, table_sem, local_sem,
-    next_send, next_recv, saved_send, saved_recv, down_send, down_recv,
-    c_send, c_recv, x_send, x_recv, cf_send, cf_recv, xf_send, xf_recv,
-    rs_send, rs_recv, rc_send, rc_recv, rx_send, rx_recv, pick_send, pick_recv,
-    bg_send, bg_recv, bo_send, bo_recv, part_send, part_recv, pre_send, pre_recv,
-    late_send, late_recv,
+    weight_sem, table_sem, local_sem, send_sem, entry_sem,
+    next_recv, saved_recv, down_recv, c_recv, x_recv, cf_recv, xf_recv,
+    rs_recv, rc_recv, rx_recv, pick_recv, bg_recv, bo_recv, part_recv, pre_recv, late_recv,
 ):
     n_pipe, ne, nt, capacity = sizes
     tokens, width = x_own.shape
     features = width * nt
     experts, blocks = send_s.shape[0], send_x.shape[0]
     folds = width // send_s.shape[2]
+    peers = ne * nt - 1
+    row_lines = BLOCK * send_s.shape[2] // 128
     me_p, me_e, me_t = lax.axis_index("pipe"), lax.axis_index("expert"), lax.axis_index("tensor")
     nxt, prv = lax.rem(me_p + 1, n_pipe), lax.rem(me_p + n_pipe - 1, n_pipe)
     my_cols = pl.ds(pl.multiple_of(me_t * width, 128), width)
@@ -92,9 +91,6 @@
         copy.start()
         return copy
 
-    def sent(whole, sem):
-        planned(whole, whole, sem, sem, {"pipe": nxt}).wait_send()
-
     def received(whole, sem):
         planned(whole, whole, sem, sem, {"pipe": nxt}).wait_recv()
 
@@ -116,9 +112,11 @@
     x_load = load(x_hbm, x_own, local_sem.at[2])
 
     barrier = pltpu.get_barrier_semaphore()
+    mate = me_e + 1 - 2 * lax.rem(me_e, 2)
     greeted = [{"pipe": nxt}, {"pipe": prv}]
-    for se in range(ne):
-        for st in range(nt):
+    for st in range(nt):
+        greeted.append({"expert": mate, "tensor": peer_t(st)})
+        for se in range(0, ne, 2):
             if se or st:
                 greeted.append({"expert": peer_e(se), "tensor": peer_t(st)})
     for device in greeted:
@@ -131,21 +129,22 @@
     down_s_load = load(down_s_hbm, down_s, weight_sem.at[4])
     down_r_load = load(down_r_hbm, down_r, weight_sem.at[5])
     pl.semaphore_wait(barrier, len(greeted))
+    pl.semaphore_signal(entry_sem, inc=1, device_id={"expert": mate}, device_id_type=MESH)
 
     pltpu.make_async_copy(tables, tables, table_sem).wait()
     for a in range(3):
-        remote(tables.at[a, 0], tables_next.at[a], next_send, next_recv, {"pipe": prv})
+        remote(tables.at[a, 0], tables_next.at[a], send_sem, next_recv, {"pipe": prv})
     c_copies = [
         planned(
             c_own.at[:, local_cols(n)], full_c.at[:, cols_of(me_t, n)],
-            c_send, c_recv.at[n], {"pipe": prv},
+            send_sem, c_recv.at[n], {"pipe": prv},
         )
         for n in range(chunks)
     ]
     x_copies = [
         planned(
             x_own.at[:, local_cols(n)], full_x.at[:, cols_of(me_t, n)],
-            x_send, x_recv.at[n], {"pipe": nxt},
+            send_sem, x_recv.at[n], {"pipe": nxt},
         )
         for n in range(chunks)
     ]
@@ -155,7 +154,7 @@
     x_load.wait()
     saved_copies = [
         remote(
-            full_s.at[:, my_cols], full_s.at[:, my_cols], saved_send.at[st - 1],
+            full_s.at[:, my_cols], full_s.at[:, my_cols], send_sem,
             saved_recv.at[st - 1], {"tensor": peer_t(st)},
         )
         for st in range(1, nt)
@@ -165,13 +164,13 @@
         to = peer_t(st)
         down_copies.append(remote(
             down_s_hbm.at[:, pl.ds(pl.multiple_of(to * width, 128), width)], down_peer.at[st - 1],
-            down_send.at[st - 1], down_recv.at[st - 1], {"tensor": to},
+            send_sem, down_recv.at[st - 1], {"tensor": to},
         ))
         for part in range(nt):
             at = pl.ds(part * width + (chunks - LATE) * cw, LATE * cw)
             for a, src in enumerate((gate_s_hbm, up_s_hbm)):
                 remote(
-                    src.at[at, :], late_w.at[a, st - 1, part], late_send, late_recv, {"tensor": to}
+                    src.at[at, :], late_w.at[a, st - 1, part], send_sem, late_recv, {"tensor": to}
                 )
 
     def table(target, values, slots_at):
@@ -201,30 +200,19 @@
         pieces = [held[f * capacity:(f + 1) * capacity] for f in range(folds)]
         return jnp.concatenate(pieces, axis=1)
 
-    def exchange(buffer, landing, ssem, rsem):
+    def exchange(buffer, landing, rsem):
         for se in range(ne):
             for st in range(nt):
                 if se or st:
-                    to_e, n = peer_e(se), min(se, 1)
+                    to_e = peer_e(se)
                     remote(
-                        buffer.at[lax.div(to_e, 2)], landing.at[me_e, me_t], ssem.at[n], rsem.at[n],
+                        buffer.at[lax.div(to_e, 2)], landing.at[me_e, me_t], send_sem, rsem,
                         {"expert": to_e, "tensor": peer_t(st)},
                     )
         landing[me_e, me_t] = buffer[lax.div(me_e, 2)]
 
-    def near(landing):
-        return landing.at[0, pl.ds(0, nt - 1)]
-
-    def far(landing):
-        return landing.at[pl.ds(0, ne - 1)]
-
-    def wait_rows(landing, rsem):
-        received(near(landing), rsem.at[0])
-        received(far(landing), rsem.at[1])
-
-    def wait_rows_sent(landing, ssem):
-        sent(near(landing), ssem.at[0])
-        sent(far(landing), ssem.at[1])
+    def wait_rows(rsem):
+        received(drain.at[pl.ds(0, peers * row_lines)], rsem)
 
     group = 16 // capacity
 
@@ -244,7 +232,8 @@
             buffer[k] = pack(picked[k * capacity:(k + 1) * capacity])
 
     fill(send_s, pick_rows(pick_b, lambda n: full_s[:, cols_of(me_t, n)]))
-    exchange(send_s, recv_s, rs_send, rs_recv)
+    pl.semaphore_wait(entry_sem, 1)
+    exchange(send_s, recv_s, rs_recv)
 
     parts = ne * nt * capacity
     place_b = lax.broadcasted_iota(jnp.int32, (parts, tokens), 0)
@@ -277,7 +266,7 @@
     picked = pick_rows(pick_n, lambda n: x_own[:, local_cols(n)])
     for b in range(blocks):
         send_x[b] = picked[b * BLOCK:(b + 1) * BLOCK].astype(BF16)
-    picked_copy = remote(send_x, held_x, pick_send, pick_recv, {"pipe": nxt})
+    picked_copy = remote(send_x, held_x, send_sem, pick_recv, {"pipe": nxt})
 
     order = [(c_copies, n) for n in range(FIRST_COT, chunks)]
     early = list(order)
@@ -309,7 +298,7 @@
     for n in range(EARLY_TURNS):
         turn(n)
 
-    wait_rows(recv_s, rs_recv)
+    wait_rows(rs_recv)
     gather_rows(recv_s)
     gate_back = dot(rows[...], gate_r[...])
     a_routed[...] = dot(rows[...], up_r[...]) * swish_slope(gate_back)
@@ -317,16 +306,22 @@
 
     down_s_load.wait()
 
-    def forward(held, n, ssem, rsem):
+    def forwards(held, n, rsem):
         cols = cols_of(me_t, n)
         return [
-            remote(
-                held.at[:, cols], held.at[:, cols], ssem.at[st - 1], rsem.at[n, st - 1],
+            planned(
+                held.at[:, cols], held.at[:, cols], send_sem, rsem.at[n, st - 1],
                 {"tensor": peer_t(st)},
             )
             for st in range(1, nt)
         ]
 
+    def forward(held, n, rsem):
+        copies = forwards(held, n, rsem)
+        for copy in copies:
+            copy.start()
+        return copies
+
     def add_cot(part, n, first=False):
         cols = cols_of(part, n)
         piece = contract_last(full_c[:, cols], down_s[:, cols])
@@ -340,7 +335,7 @@
     cf_copies = []
     for n in range(chunks):
         c_copies[n].wait_recv()
-        cf_copies.append(forward(full_c, n, cf_send, cf_recv))
+        cf_copies.append(forward(full_c, n, cf_recv))
         if n == INPUT_GATE:
             @pl.when(me_p != last_p)
             def _():
@@ -351,13 +346,13 @@
                 x_copies[m].start()
         if n == chunks - 1:
             fill(send_c, scale_b * pick_rows(pick_b, lambda m: full_c[:, cols_of(me_t, m)]))
-            exchange(send_c, recv_c, rc_send, rc_recv)
+            exchange(send_c, recv_c, rc_recv)
         if n == RELAY_AT:
             picked_copy.wait_recv()
             for k in range(experts):
                 b, at = divmod(k * capacity, BLOCK)
                 relay_x[k] = pack(held_x[b].astype(F32)[at:at + capacity])
-            exchange(relay_x, recv_x, rx_send, rx_recv)
+            exchange(relay_x, recv_x, rx_recv)
         add_cot(me_t, n, first=n == 0)
         if n + EARLY_TURNS < chunks:
             turn(n + EARLY_TURNS)
@@ -367,9 +362,9 @@
 
     def land_in(n):
         x_copies[n].wait_recv()
-        xf_copies.append(forward(full_x, n, xf_send, xf_recv))
-
-    def send_back(total_of, buffer, landing, ssem, rsem):
+        xf_copies.append(forward(full_x, n, xf_recv))
+
+    def send_back(total_of, buffer, landing, rsem):
         for st in list(range(1, nt)) + [0]:
             to_t = peer_t(st)
             total = jnp.concatenate([total_of(cols_of(to_t, n)) for n in range(chunks)], axis=1)
@@ -377,9 +372,9 @@
                 buffer[i, to_t] = pack(total[i * capacity:(i + 1) * capacity])
             for se in range(ne):
                 if se or st:
-                    to_e, n = peer_e(se), min(se, 1)
+                    to_e = peer_e(se)
                     remote(
-                        buffer.at[to_e, to_t], landing.at[me_e, me_t], ssem.at[n], rsem.at[n],
+                        buffer.at[to_e, to_t], landing.at[me_e, me_t], send_sem, rsem,
                         {"expert": to_e, "tensor": to_t},
                     )
         landing[me_e, me_t] = buffer[me_e, me_t]
@@ -397,26 +392,26 @@
             )
         if st:
             part_copies.append(remote(
-                part_grad.at[st], peer_grad.at[st - 1], part_send.at[st - 1],
+                part_grad.at[st], peer_grad.at[st - 1], send_sem,
                 part_recv.at[st - 1], {"tensor": to},
             ))
     land_in(0)
 
-    wait_rows(recv_x, rx_recv)
+    wait_rows(rx_recv)
     gather_rows(recv_x)
     gate_fwd = dot(rows[...], gate_r[...])
     hidden_r = (swish(gate_fwd) * dot(rows[...], up_r[...])).astype(BF16)
     send_back(
-        lambda cols: dot(hidden_r, down_r[:, cols]), back_send_o, back_recv_o, bo_send, bo_recv
+        lambda cols: dot(hidden_r, down_r[:, cols]), back_send_o, back_recv_o, bo_recv
     )
-    wait_rows(recv_c, rc_recv)
+    wait_rows(rc_recv)
     gather_rows(recv_c)
     grad_back = dot(rows[...], down_rt[...])
     gate_grad_r = (grad_back * a_routed[...]).astype(BF16)
     up_grad_r = (grad_back * b_routed[...]).astype(BF16)
     send_back(
         lambda cols: dot(gate_grad_r, gate_rt[:, cols]) + dot(up_grad_r, up_rt[:, cols]),
-        back_send_g, back_recv_g, bg_send, bg_recv,
+        back_send_g, back_recv_g, bg_recv,
     )
     land_in(1)
 
@@ -430,7 +425,7 @@
             )
 
     def finish_grad():
-        wait_rows(back_recv_g, bg_recv)
+        wait_rows(bg_recv)
         gather_back(back_recv_g)
         for copy in part_copies:
             copy.wait_recv()
@@ -458,45 +453,32 @@
 
     for n in range(3, early_n - 1):
         land_in(n)
-    for n in range(early_n - 1):
-        arrived(n)
-    add_in([(source_t(st), n) for n in range(early_n - 1) for st in range(nt)], first=True)
-    land_in(early_n - 1)
-    land_in(early_n)
-    add_in([(me_t, early_n - 1)])
-    arrived(early_n - 1)
-    add_in([(source_t(st), early_n - 1) for st in range(1, nt)])
-
-    pre_copies = [
-        remote(
-            pre, pre_peer.at[st - 1], pre_send.at[st - 1], pre_recv.at[st - 1],
-            {"tensor": peer_t(st)},
-        )
-        for st in range(1, nt)
-    ]
-    wait_rows(back_recv_o, bo_recv)
+    wait_rows(bo_recv)
     gather_back(back_recv_o)
     for n in range(chunks):
         at = local_cols(n)
         held = back_rows[:, at]
         out_sum[:, at] = dot(factor_high[...], held) + dot(factor_low[...], held)
+    for n in range(early_n - 1):
+        arrived(n)
+    add_in([(source_t(st), n) for n in range(early_n - 1) for st in range(nt)], first=True)
+    land_in(early_n - 1)
     finish_grad()
+    land_in(early_n)
+    add_in([(me_t, early_n - 1)])
+    arrived(early_n - 1)
+    add_in([(source_t(st), early_n - 1) for st in range(1, nt)])
+
+    pre_copies = [
+        remote(
+            pre, pre_peer.at[st - 1], send_sem, pre_recv.at[st - 1], {"tensor": peer_t(st)},
+        )
+        for st in range(1, nt)
+    ]
     for copy in down_copies:
         copy.wait_recv()
     received(late_w, late_recv)
-    sent(c_own, c_send)
-    sent(tables_next, next_send)
-    sent(send_x, pick_send)
-    for landing, sem in (
-        (recv_s, rs_send), (recv_c, rc_send), (recv_x, rx_send),
-        (back_recv_g, bg_send), (back_recv_o, bo_send),
-    ):
-        wait_rows_sent(landing, sem)
-    sent(late_w, late_send)
-    for copy in saved_copies + down_copies + part_copies:
-        copy.wait_send()
-    for st in range(1, nt):
-        sent(full_c.at[:, my_cols], cf_send.at[st - 1])
+
     def late_piece(unit, a, part, n):
         cols = cols_of(part, n)
         if unit:
@@ -504,16 +486,34 @@
             return dot(full_x[:, cols], late_w[a, unit - 1, part, at:at + cw, :])
         return dot(full_x[:, cols], (gate_s, up_s)[a][cols, :])
 
-    for n in range(early_n, chunks - 1):
-        arrived(n)
-    for unit in range(nt):
-        for a in range(2):
-            total = pre[a] if unit == 0 else 0.0
-            for n in range(early_n, chunks - 1):
-                for st in range(nt):
-                    total = total + late_piece(unit, a, source_t(st), n)
-            late[unit, a] = total
-    land_in(chunks - 1)
+    xf_copies.append(forwards(full_x, chunks - 1, xf_recv))
+
+    def land_last():
+        x_copies[chunks - 1].wait_recv()
+        for copy in xf_copies[chunks - 1]:
+            copy.start()
+
+    def add_late():
+        for n in range(early_n, chunks - 1):
+            arrived(n)
+        for unit in range(nt):
+            for a in range(2):
+                total = pre[a] if unit == 0 else 0.0
+                for n in range(early_n, chunks - 1):
+                    for st in range(nt):
+                        total = total + late_piece(unit, a, source_t(st), n)
+                late[unit, a] = total
+
+    @pl.when(lax.rem(me_t, 2) == 0)
+    def _():
+        add_late()
+        land_last()
+
+    @pl.when(lax.rem(me_t, 2) != 0)
+    def _():
+        land_last()
+        add_late()
+
     for unit in range(nt):
         for a in range(2):
             late[unit, a] = late[unit, a] + late_piece(unit, a, me_t, chunks - 1)
@@ -535,11 +535,7 @@
             total = total + dot(hidden[st], down_peer[st - 1, :, at])
         out_ref[:, at] = total.astype(BF16)
 
-    sent(x_own, x_send)
-    for st in range(1, nt):
-        sent(full_x.at[:, my_cols], xf_send.at[st - 1])
-    for copy in pre_copies:
-        copy.wait_send()
+    planned(drain, drain, send_sem, send_sem, {"pipe": nxt}).wait_send()
 
 
 def store(out, grad, out_hbm, grad_hbm, sem):
@@ -574,6 +570,16 @@
     fr, fs = gate_routed.shape[3], gate_shared.shape[2]
     chunks = width // chunk_of(width)
     peers = ne * nt - 1
+    sent_bytes = (
+        3 * topk * tokens * 4
+        + (2 + 3 * (nt - 1)) * tokens * width * 2
+        + (nt - 1) * fs * width * 2
+        + 2 * (nt - 1) * nt * LATE * chunk_of(width) * fs * 2
+        + 5 * peers * BLOCK * folded * 2
+        + blocks * BLOCK * width * 2
+        + (nt - 1) * tokens * width * 4
+        + (nt - 1) * 2 * tokens * fs * 4
+    )
     vmem = pl.BlockSpec(memory_space=pltpu.VMEM)
     hbm = pl.BlockSpec(memory_space=pl.ANY)
     dma = pltpu.SemaphoreType.DMA
@@ -606,6 +612,7 @@
             pltpu.VMEM((nt, 2, tokens, fs), F32),
             pltpu.VMEM((2, nt - 1, nt, LATE * chunk_of(width), fs), BF16),
             pltpu.VMEM((nt, tokens, fs), BF16),
+            pltpu.VMEM((sent_bytes // 256, 128), BF16),
             pltpu.VMEM((tokens, fs), BF16),
             pltpu.VMEM((tokens, fs), BF16),
             pltpu.VMEM((ne * capacity, fr), F32),
@@ -635,17 +642,10 @@
             pltpu.VMEM((tokens, ne * nt * capacity), BF16),
             pltpu.VMEM((tokens, ne * nt * capacity), BF16),
             pltpu.VMEM((tokens, ne * nt * capacity), BF16),
-            dma((6,)), dma, dma((3,)),
-            dma, dma,
-            dma((nt - 1,)), dma((nt - 1,)), dma((nt - 1,)), dma((nt - 1,)),
-            dma, dma((chunks,)), dma, dma((chunks,)),
-            dma((nt - 1,)), dma((chunks, nt - 1)),
-            dma((nt - 1,)), dma((chunks, nt - 1)),
-            dma((2,)), dma((2,)), dma((2,)), dma((2,)),
-            dma((2,)), dma((2,)), dma, dma,
-            dma((2,)), dma((2,)), dma((2,)), dma((2,)),
-            dma((nt - 1,)), dma((nt - 1,)), dma((nt - 1,)), dma((nt - 1,)),
-            dma, dma,
+            dma((6,)), dma, dma((3,)), dma, pltpu.SemaphoreType.REGULAR,
+            dma, dma((nt - 1,)), dma((nt - 1,)), dma((chunks,)), dma((chunks,)),
+            dma((chunks, nt - 1)), dma((chunks, nt - 1)),
+            dma, dma, dma, dma, dma, dma, dma((nt - 1,)), dma((nt - 1,)), dma,
         ],
         compiler_params=pltpu.CompilerParams(
             collective_id=0, has_side_effects=True, vmem_limit_bytes=60 * 1024 * 1024

time: 33.9 us -> 32.3 us (0.953)
  Pallas kernels: 33.1 us -> 31.2 us
    pallas_call x1, Pallas kernels: 32.2 us -> 30.3 us  [local(): pl.pallas_call(functools.partial(kernel, (n_pipe, ne, nt, capacity)), out...]
where the time goes in v3:
time: 32.3 us; the launch traced here: 31.9 us
  Pallas kernels  31.2 us (97%)
  between operations  0.64 us (2%)
    pallas_call x1, Pallas kernels, local(): pl.pallas_call(functools.partial(kernel, (n_pipe, ne, nt, capacity)), out...  30.3 us
    pallas_call x1, Pallas kernels, local(): pl.pallas_call(store, out_shape=(result, result), in_specs=[vmem] * 2, ou...  0.94 us

profile of v3, /device:TPU:0, one launch (start us, length us, event | category | flops | bytes accessed | tf_op | source)
XLA Modules:
  0.0 31.9 jit_solution(10158506447969851536)
XLA Ops:
  0.6 30.3 %moe_step.1 = (bf16[128,1792]{1,0:T(8,128)(2,1)S(1)}, bf16[128,1792]{1,0:T(8,128)(2,1)S(1)}) custom-call(bf16[128,1792]{1,0:T(8,128)(2,1)} %bitcast.29, bf16[128,1792]{1,0:T(8,128)(2,1)} %bitcast.30, bf16[128,1792]{1,0:T(8,128)(2,1)} %bitcast.31, s32[2,8,128]{2,1,0:T(8,128)} %bitcast.32, s32[2,8,128]{2,1,0:T(8,128)} %bitcast.33, s32[2,8,128]{2,1,0:T(8,128)} %bitcast.34, ...), custom_call_target="tpu_custom_call" | custom-call | tf_op jit(solution)/shard_map/moe_step/pallas_call | solution.py:587
  30.9 0.9 %store_out.1 = (bf16[128,1792]{1,0:T(8,128)(2,1)}, bf16[128,1792]{1,0:T(8,128)(2,1)}) custom-call(bf16[128,1792]{1,0:T(8,128)(2,1)S(1)} %get-tuple-element.6.out, bf16[128,1792]{1,0:T(8,128)(2,1)S(1)} %get-tuple-element.7.grad), custom_call_target="tpu_custom_call" | custom-call | tf_op jit(solution)/shard_map/store_out/pallas_call | solution.py:663

commit v4 on v3

--- a/solution.py
+++ b/solution.py
@@ -310,7 +310,7 @@
         cols = cols_of(me_t, n)
         return [
             planned(
-                held.at[:, cols], held.at[:, cols], send_sem, rsem.at[n, st - 1],
+                held.at[:, cols], held.at[:, cols], send_sem, rsem(n).at[st - 1],
                 {"tensor": peer_t(st)},
             )
             for st in range(1, nt)
@@ -335,7 +335,7 @@
     cf_copies = []
     for n in range(chunks):
         c_copies[n].wait_recv()
-        cf_copies.append(forward(full_c, n, cf_recv))
+        cf_copies.append(forward(full_c, n, lambda m: cf_recv.at[m]))
         if n == INPUT_GATE:
             @pl.when(me_p != last_p)
             def _():
@@ -360,9 +360,12 @@
             add_forwarded(cf_copies[n - 1], n - 1, add_cot)
     xf_copies = []
 
+    def input_sem(n):
+        return xf_recv.at[max(n - (chunks - LATE - 2), 0)]
+
     def land_in(n):
         x_copies[n].wait_recv()
-        xf_copies.append(forward(full_x, n, xf_recv))
+        xf_copies.append(forward(full_x, n, input_sem))
 
     def send_back(total_of, buffer, landing, rsem):
         for st in list(range(1, nt)) + [0]:
@@ -459,8 +462,8 @@
         at = local_cols(n)
         held = back_rows[:, at]
         out_sum[:, at] = dot(factor_high[...], held) + dot(factor_low[...], held)
-    for n in range(early_n - 1):
-        arrived(n)
+    for st in range(1, nt):
+        received(full_x.at[:, pl.ds(0, (early_n - 1) * cw)], xf_recv.at[0, st - 1])
     add_in([(source_t(st), n) for n in range(early_n - 1) for st in range(nt)], first=True)
     land_in(early_n - 1)
     finish_grad()
@@ -486,7 +489,7 @@
             return dot(full_x[:, cols], late_w[a, unit - 1, part, at:at + cw, :])
         return dot(full_x[:, cols], (gate_s, up_s)[a][cols, :])
 
-    xf_copies.append(forwards(full_x, chunks - 1, xf_recv))
+    xf_copies.append(forwards(full_x, chunks - 1, input_sem))
 
     def land_last():
         x_copies[chunks - 1].wait_recv()
@@ -644,7 +647,7 @@
             pltpu.VMEM((tokens, ne * nt * capacity), BF16),
             dma((6,)), dma, dma((3,)), dma, pltpu.SemaphoreType.REGULAR,
             dma, dma((nt - 1,)), dma((nt - 1,)), dma((chunks,)), dma((chunks,)),
-            dma((chunks, nt - 1)), dma((chunks, nt - 1)),
+            dma((chunks, nt - 1)), dma((LATE + 2, nt - 1)),
             dma, dma, dma, dma, dma, dma, dma((nt - 1,)), dma((nt - 1,)), dma,
         ],
         compiler_params=pltpu.CompilerParams(

time: 32.3 us -> 32.3 us (level)
  no operation moved by 1% of the time
where the time goes in v4:
time: 32.3 us; the launch traced here: 31.9 us
  Pallas kernels  31.2 us (97%)
  between operations  0.64 us (2%)
    pallas_call x1, Pallas kernels, local(): pl.pallas_call(functools.partial(kernel, (n_pipe, ne, nt, capacity)), out...  30.3 us
    pallas_call x1, Pallas kernels, local(): pl.pallas_call(store, out_shape=(result, result), in_specs=[vmem] * 2, ou...  0.94 us

profile of v4, /device:TPU:0, one launch (start us, length us, event | category | flops | bytes accessed | tf_op | source)
XLA Modules:
  0.0 31.9 jit_solution(16096277498656532530)
XLA Ops:
  0.6 30.3 %moe_step.1 = (bf16[128,1792]{1,0:T(8,128)(2,1)S(1)}, bf16[128,1792]{1,0:T(8,128)(2,1)S(1)}) custom-call(bf16[128,1792]{1,0:T(8,128)(2,1)} %bitcast.29, bf16[128,1792]{1,0:T(8,128)(2,1)} %bitcast.30, bf16[128,1792]{1,0:T(8,128)(2,1)} %bitcast.31, s32[2,8,128]{2,1,0:T(8,128)} %bitcast.32, s32[2,8,128]{2,1,0:T(8,128)} %bitcast.33, s32[2,8,128]{2,1,0:T(8,128)} %bitcast.34, ...), custom_call_target="tpu_custom_call" | custom-call | tf_op jit(solution)/shard_map/moe_step/pallas_call | solution.py:590
  30.9 0.9 %store_out.1 = (bf16[128,1792]{1,0:T(8,128)(2,1)}, bf16[128,1792]{1,0:T(8,128)(2,1)}) custom-call(bf16[128,1792]{1,0:T(8,128)(2,1)S(1)} %get-tuple-element.6.out, bf16[128,1792]{1,0:T(8,128)(2,1)S(1)} %get-tuple-element.7.grad), custom_call_target="tpu_custom_call" | custom-call | tf_op jit(solution)/shard_map/store_out/pallas_call | solution.py:666
